TPU v7x, 128 devices: a whole 4x4x4 slice. The times are simulated.
128 devices in a mesh: member: 2 (over core), grid: 64 (over z, y, x).
Axes of the slice: x: 4, y: 4, z: 4, core: 2. Of those that a mesh axis runs over, the one named last changes fastest.
Arguments:
- latent: bfloat16 [4, 131072, 512], P('member', 'grid'), may hold values from -80 to 80
- block_pick: int32 [64, 64], P('grid'), may hold values from 0 to 15
- obs_weight: bfloat16 [64, 64, 32, 128], P('grid'), may hold values from 0.0099487305 to 1
- obs_value: float32 [64, 64, 32, 128], P('grid'), may hold values from -6 to 6
- obs_count: int32 [64, 64], P('grid'), may hold values from 0 to 32, as said below
- w_in: bfloat16 [512, 512], replicated, may hold values from -0.25 to 0.25
- b_in: float32 [512], replicated, may hold values from -3 to 3
- w_out: bfloat16 [512, 128], replicated, may hold values from -0.25 to 0.25
- b_out: float32 [128], replicated, may hold values from -3 to 3
Outputs:
- latent_grad: float32 [4, 131072, 512], P('member', 'grid')
- loss_value: float32 [], replicated
Inputs may be any that keep to these rules, and one draw needn't show every extreme that they name: Entry [d, j] counts the live observations of those slots; the live ones are the first slots, k < obs_count[d, j].
All inputs are finite; a program needn't handle non-finite values.
Results may differ from a plain program's by a relative error of at most 0.0041.
Values may be sent and summed in bfloat16 or wider, within the bound.
No kernel may reach another device: no remote copies, remote signals or barrier semaphores. Data moves between devices by JAX's collectives and lax.ppermute only.
A program may use at most 128 MiB of HBM per device.

v0:
```python
import jax
import jax.numpy as jnp
from jax import lax
from jax.sharding import Mesh
from jax.sharding import PartitionSpec as P

GRID = ("grid_0", "grid_1", "grid_2")
MEMBER_GRID = ("member", "grid_0", "grid_1", "grid_2")


SOFTEN = 0.1


def sent_to_all(value, axis):
    copies = jnp.broadcast_to(value, (lax.axis_size(axis), *value.shape))
    return lax.all_to_all(copies, axis, split_axis=0, concat_axis=0, tiled=True)


def taken_together(value, axis):
    everything = sent_to_all(value, axis)
    return jnp.sum(everything, axis=0)


def one_axis_at_a_time(value, axes):
    for axis in axes:
        value = lax.psum(value, axis)
    return value


def smooth_abs(value):
    return jnp.sqrt(value * value + SOFTEN * SOFTEN)


def silu_slope(pre_act):
    sigmoid_value = jax.nn.sigmoid(pre_act)
    return sigmoid_value * (1.0 + pre_act * (1.0 - sigmoid_value))


def per_device(latent, block_pick, obs_weight, obs_value, obs_count, w_in, b_in, w_out, b_out):
    members_here, points, feature_width = latent.shape
    peer_count = lax.axis_size(GRID)
    slot_count = obs_weight.shape[2]
    block_size = obs_weight.shape[3]
    channels = obs_value.shape[3]
    members_all = members_here * lax.axis_size("member")
    block_count = points // block_size
    local_blocks = latent.reshape(members_here, block_count, block_size, feature_width)
    picked_ids = block_pick[0]
    block_onehot = (
        picked_ids[:, None] == jnp.arange(block_count, dtype=jnp.int32)[None, :]
    ).astype(jnp.bfloat16)
    weight_sum = jnp.sum(obs_weight[0], axis=2, keepdims=True, dtype=jnp.float32)
    norm_weight = (obs_weight[0] / weight_sum).astype(jnp.bfloat16)
    picked = local_blocks[:, picked_ids]
    owner_weight = lax.all_to_all(norm_weight, GRID, split_axis=0, concat_axis=0, tiled=True)
    owner_interp = jnp.einsum(
        "dkp,mdpc->mdkc", owner_weight, picked, preferred_element_type=jnp.float32
    ).astype(jnp.bfloat16)
    interp = lax.all_to_all(owner_interp, GRID, split_axis=1, concat_axis=1, tiled=True)
    flat_rows = interp.reshape(members_here * peer_count * slot_count, feature_width)
    pre_act = jnp.dot(flat_rows, w_in, preferred_element_type=jnp.float32) + b_in
    hidden = jax.nn.silu(pre_act).astype(jnp.bfloat16)
    predicted = jnp.dot(hidden, w_out, preferred_element_type=jnp.float32) + b_out
    predicted = predicted.reshape(members_here, peer_count, slot_count, channels)
    all_members = lax.all_gather(predicted, "member", axis=0, tiled=True)
    target = obs_value[0]
    live_mask = (jnp.arange(slot_count, dtype=jnp.int32)[None, :] < obs_count[0][:, None]).astype(
        jnp.float32
    )
    obs_diff = predicted - target[None]
    pair_diff = predicted[:, None] - all_members[None]
    per_obs = smooth_abs(obs_diff) / members_all - jnp.sum(smooth_abs(pair_diff), axis=1) / (
        2.0 * members_all * (members_all - 1)
    )
    loss_part = jnp.sum(per_obs * live_mask[None, :, :, None])
    live_count = jnp.sum(live_mask)
    live_total = taken_together(live_count, GRID)
    loss_total = one_axis_at_a_time(loss_part, MEMBER_GRID)
    loss_value = loss_total / (channels * live_total)
    grad_scale = peer_count * peer_count * slot_count / live_total
    slope_obs = obs_diff / smooth_abs(obs_diff)
    slope_pair = jnp.sum(pair_diff / smooth_abs(pair_diff), axis=1)
    grad_pred = (
        grad_scale
        * live_mask[None, :, :, None]
        * (slope_obs / members_all - slope_pair / (members_all * (members_all - 1.0)))
    ).astype(jnp.bfloat16)
    grad_hidden = jnp.einsum(
        "rv,hv->rh", grad_pred.reshape(-1, channels), w_out, preferred_element_type=jnp.float32
    )
    grad_act = (grad_hidden * silu_slope(pre_act)).astype(jnp.bfloat16)
    grad_interp = jnp.einsum(
        "rh,ch->rc", grad_act, w_in, preferred_element_type=jnp.float32
    ).astype(jnp.bfloat16)
    grad_interp = grad_interp.reshape(members_here, peer_count, slot_count, feature_width)
    owner_grad = lax.all_to_all(grad_interp, GRID, split_axis=1, concat_axis=1, tiled=True)
    returned = jnp.einsum(
        "dkp,mdkc->mdpc", owner_weight, owner_grad, preferred_element_type=jnp.float32
    ).astype(jnp.bfloat16)
    summed = jnp.einsum("mdpc,db->mbpc", returned, block_onehot, preferred_element_type=jnp.float32)
    latent_grad = summed.reshape(members_here, points, feature_width)
    return (latent_grad, loss_value)


def solution(mesh):
    split = Mesh(
        mesh.devices.reshape(mesh.shape["member"], 4, 4, 4),
        ("member", "grid_0", "grid_1", "grid_2"),
    )
    return jax.shard_map(
        per_device,
        mesh=split,
        in_specs=(
            P("member", GRID, None),
            P(GRID, None),
            P(GRID, None, None, None),
            P(GRID, None, None, None),
            P(GRID, None),
            P(),
            P(),
            P(),
            P(),
        ),
        out_specs=(P("member", GRID, None), P()),
        check_vma=False,
    )
```

profile of v0, /device:TPU:1, one launch (start us, length us, event | category | flops | bytes accessed | tf_op | source)
XLA Modules:
  0.0 285.4 jit_solution(11307042710669002750)
XLA Ops:
  7.2 0.0 copy-start
  7.2 1.4 convert_reduce_fusion
  8.6 2.2 fusion.13
  10.8 12.0 %all-to-all-start.1 = ((bf16[64,32,128]{2,1,0:T(8,128)(2,1)}), bf16[64,32,128]{2,1,0:T(8,128)(2,1)S(1)}, u32[]{:S(2)}, u32[]{:S(2)}) async-start(bf16[64,32,128]{2,1,0:T(8,128)(2,1)} %fusion.13), calls=%async_computation.1 | async-start | bytes 1048576 | tf_op jit(solution)/shard_map/all_to_all | solution.py:55
  22.8 0.0 all-gather.2.cloned.1.call-start
  22.8 0.7 fusion.22
  23.5 9.8 %gather_fusion = bf16[64,2,128,512]{3,2,1,0:T(8,128)(2,1)} fusion(bf16[2,16,128,512]{3,2,1,0:T(8,128)(2,1)} %bitcast.67, s32[1024]{0:T(1024)S(1)} %pad_clamp_fusion), kind=kCustom, calls=%fused_computation | custom fusion | bytes 33554688 | tf_op jit(solution)/shard_map/gather | solution.py:54
  33.2 1.7 all-to-all-done.1
  34.9 8.1 %convert_bitcast_fusion.1 = bf16[2,64,32,512]{3,2,0,1:T(8,128)(2,1)S(1)} fusion(bf16[64,2,128,512]{3,2,1,0:T(8,128)(2,1)} %gather_fusion, bf16[64,32,128]{2,1,0:T(8,128)(2,1)S(1)} %all-to-all-done.1), kind=kOutput, calls=%fused_computation.15 | convolution fusion | flops 538968064 | bytes 21495808 | tf_op jit(solution)/shard_map/dkp,mdpc->mdkc/dot_general | solution.py:56
  43.1 58.4 %all_to_all.21 = bf16[2,64,32,512]{3,2,0,1:T(8,128)(2,1)S(1)} all-to-all(bf16[2,64,32,512]{3,2,0,1:T(8,128)(2,1)S(1)} %convert_bitcast_fusion.1), channel_id=1, replica_groups=mesh['member'=2,'grid_0'=4,'grid_1'=4,'grid_2'=4] {'grid_0','grid_1','gr..., dimensions={1} | all-to-all | bytes 8388608 | tf_op jit(solution)/shard_map/all_to_all | solution.py:59
  101.4 0.6 copy.22
  102.0 0.0 copy-done
  102.0 0.0 copy-start.7
  102.0 0.0 copy-start.8
  102.0 0.0 copy-start.9
  102.0 2.4 fusion.25
  104.5 0.0 copy-done.7
  104.5 0.0 copy-done.8
  104.5 0.0 copy-done.9
  104.5 0.0 copy-start.3
  104.5 0.0 copy-start.5
  104.5 4.1 %convolution_add_fusion = f32[4096,128]{1,0:T(8,128)} fusion(bf16[512,128]{1,0:T(8,128)(2,1)S(1)} %copy-done.7, f32[4096,512]{1,0:T(8,128)S(1)} %fusion.25, f32[512]{0:T(512)S(1)} %copy-done.8, f32[128]{0:T(128)S(1)} %copy-done.9), kind=kOutput, calls=%fused_computation.14 | convolution fusion | flops 549978112 | bytes 10619392 | tf_op jit(solution)/shard_map/dot_general | solution.py:63
  108.6 0.0 copy-done.3
  108.6 0.0 all-gather.2.cloned.1.call-update
  108.6 0.0 copy-done.5
  108.6 0.7 fusion.18
  109.3 1.3 broadcast_in_dim.2
  110.6 7.6 %all-to-all-start = ((f32[64,1,1]{2,1,0:T(1,128)}), f32[64,1,1]{2,1,0:T(1,128)S(1)}, u32[]{:S(2)}, u32[]{:S(2)}) async-start(f32[64,1,1]{2,1,0:T(1,128)} %broadcast_in_dim.2), calls=%async_computation | async-start | bytes 65536 | tf_op jit(solution)/shard_map/all_to_all | solution.py:16
  118.2 0.1 fusion.17
  118.3 0.1 mul.70
  118.4 8.1 %all-to-all-done = f32[64,1,1]{2,1,0:T(1,128)S(1)} async-done(((f32[64,1,1]{2,1,0:T(1,128)}), f32[64,1,1]{2,1,0:T(1,128)S(1)}, u32[]{:S(2)}, u32[]{:S(2)}) %all-to-all-start) | async-done | bytes 288 | tf_op jit(solution)/shard_map/all_to_all | solution.py:16
  126.4 0.7 reduce_sum.55
  127.8 0.1 fusion.16
  127.9 0.1 mul.60
  128.0 0.0 all-gather.2.cloned.1.call-done
  128.0 7.4 %fusion.4 = (f32[2,64,32,128]{3,2,1,0:T(8,128)S(1)}, f32[2,64,32,128]{3,2,1,0:T(8,128)S(1)}) fusion(f32[4,64,32,128]{3,2,1,0:T(8,128)} %all-gather.2.cloned.1.call-done, f32[2,64,32,128]{3,2,1,0:T(8,128)} %bitcast.69), kind=kLoop, calls=%fused_computation.8 | loop fusion | flops 11534336 | bytes 10485760 | tf_op jit(solution)/shard_map/reduce_sum | solution.py:72
  135.4 0.0 copy-start.2
  135.4 0.0 copy-start.4
  135.4 0.5 broadcast_multiply_fusion
  136.0 1.0 copy-done.2
  137.0 0.3 copy-done.4
  137.3 2.5 fusion.9
  139.8 8.6 %convolution_convert_fusion = bf16[4096,512]{1,0:T(8,128)(2,1)} fusion(bf16[512,512]{1,0:T(8,128)(2,1)S(1)} %copy-done, f32[4096,512]{1,0:T(8,128)} %copy-done.3, bf16[4096,128]{1,0:T(8,128)(2,1)S(1)} %get-tuple-element.5, bf16[512,128]{1,0:T(8,128)(2,1)S(1)} %copy-done.7, f32[512]{0:T(512)S(1)} %copy-done.8), kind=kOutput, calls=%fused_computation.13 | convolution fusion | flops 2707423232 | bytes 14288896 | tf_op jit(solution)/shard_map/rh,ch->rc/dot_general | solution.py:92
  148.4 4.8 %copy.23 = bf16[2,64,32,512]{3,2,0,1:T(8,128)(2,1)} copy(bf16[2,64,32,512]{3,2,1,0:T(8,128)(2,1)} %bitcast.72) | data formatting | bytes 8388608 | tf_op jit(solution)/shard_map/reshape | solution.py:95
  153.2 6.9 %all-to-all-start.3 = ((bf16[2,64,32,512]{3,2,0,1:T(8,128)(2,1)}), bf16[2,64,32,512]{3,2,0,1:T(8,128)(2,1)}, u32[]{:S(2)}, u32[]{:S(2)}) async-start(bf16[2,64,32,512]{3,2,0,1:T(8,128)(2,1)} %copy.23), calls=%async_computation.3 | async-start | bytes 8388608 | tf_op jit(solution)/shard_map/all_to_all | solution.py:96
  160.1 3.8 %psum.28 = f32[]{:T(128)} all-reduce(f32[]{:T(128)} %get-tuple-element.4), channel_id=1, replica_groups=mesh['member'=2,'grid_0'=4,'grid_1'=4,'grid_2'=4] {'member'}, use_global_device_ids=true, to_apply=%region_6.7 | all-reduce | flops 1 | bytes 8 | tf_op jit(solution)/shard_map/psum | solution.py:26
  164.0 24.4 %psum.29 = f32[]{:T(128)} all-reduce(f32[]{:T(128)} %psum.28), channel_id=1, replica_groups=mesh['member'=2,'grid_0'=4,'grid_1'=4,'grid_2'=4] {'grid_0'}, use_global_device_ids=true, to_apply=%region_7.8 | all-reduce | flops 1 | bytes 8 | tf_op jit(solution)/shard_map/psum | solution.py:26
  188.4 32.5 %psum.30 = f32[]{:T(128)} all-reduce(f32[]{:T(128)} %psum.29), channel_id=1, replica_groups=mesh['member'=2,'grid_0'=4,'grid_1'=4,'grid_2'=4] {'grid_1'}, use_global_device_ids=true, to_apply=%region_8.9 | all-reduce | flops 1 | bytes 8 | tf_op jit(solution)/shard_map/psum | solution.py:26
  221.6 6.7 %psum.31 = f32[]{:T(128)} all-reduce(f32[]{:T(128)} %psum.30), channel_id=1, replica_groups=mesh['member'=2,'grid_0'=4,'grid_1'=4,'grid_2'=4] {'grid_2'}, use_global_device_ids=true, to_apply=%region_9.10 | all-reduce | flops 1 | bytes 8 | tf_op jit(solution)/shard_map/psum | solution.py:26
  229.0 0.0 all-to-all-done.3
  229.0 9.8 %convert_bitcast_fusion = bf16[2,64,128,512]{2,3,0,1:T(8,128)(2,1)} fusion(bf16[2,64,32,512]{3,2,0,1:T(8,128)(2,1)} %all-to-all-done.3, bf16[64,32,128]{2,1,0:T(8,128)(2,1)S(1)} %all-to-all-done.1), kind=kOutput, calls=%fused_computation.3 | convolution fusion | flops 545259520 | bytes 21495808 | tf_op jit(solution)/shard_map/dkp,mdkc->mdpc/dot_general | solution.py:97
  238.7 0.0 copy-start.6
  238.7 23.4 %copy.24 = bf16[2,64,128,512]{3,1,2,0:T(8,128)(2,1)} copy(bf16[2,64,128,512]{2,3,0,1:T(8,128)(2,1)} %convert_bitcast_fusion) | data formatting | bytes 33554432 | tf_op jit(solution)/shard_map/convert_element_type | solution.py:99
  262.2 0.0 copy-done.6
  262.2 7.0 %convolution_bitcast_fusion = f32[2,16,128,512]{3,1,2,0:T(8,128)S(1)} fusion(bf16[2,64,128,512]{3,1,2,0:T(8,128)(2,1)} %copy.24, s32[64]{0:T(128)S(1)} %bitcast.77), kind=kOutput, calls=%fused_computation.16 | convolution fusion | flops 268436480 | bytes 25166080 | tf_op jit(solution)/shard_map/mdpc,db->mbpc/dot_general | solution.py:100
  269.2 0.0 copy-start.1
  269.2 8.3 %copy.25 = f32[2,16,128,512]{3,2,1,0:T(8,128)} copy(f32[2,16,128,512]{3,1,2,0:T(8,128)S(1)} %convolution_bitcast_fusion) | data formatting | bytes 16777216 | tf_op jit(solution)/shard_map/mdpc,db->mbpc/transpose | solution.py:100
  277.4 0.0 copy-done.1
  (3 shorter events, 0.0 us)
Async XLA Ops:
  7.2 94.8 %copy-start = (bf16[512,512]{1,0:T(8,128)(2,1)S(1)}, bf16[512,512]{1,0:T(8,128)(2,1)}, u32[]{:S(2)}) copy-start(bf16[512,512]{1,0:T(8,128)(2,1)} %param.14) | copy-start | bytes 1572868
  10.8 24.1 %all-to-all-start.1 = ((bf16[64,32,128]{2,1,0:T(8,128)(2,1)}), bf16[64,32,128]{2,1,0:T(8,128)(2,1)S(1)}, u32[]{:S(2)}, u32[]{:S(2)}) async-start(bf16[64,32,128]{2,1,0:T(8,128)(2,1)} %fusion.13), calls=%async_computation.1 | async-start | bytes 1048576 | tf_op jit(solution)/shard_map/all_to_all | solution.py:55
  22.8 105.2 %all-gather.2.cloned.1.call-start = ((), (), s32[]{:S(2)}) async-start(), calls=%async_computation.4 | async-start | bytes 6291456 | tf_op jit(solution)/shard_map/all_gather | solution.py:65
  102.0 2.5 copy-start.7
  102.0 2.5 copy-start.8
  102.0 2.5 copy-start.9
  104.5 4.1 %copy-start.3 = (f32[4096,512]{1,0:T(8,128)}, f32[4096,512]{1,0:T(8,128)S(1)}, u32[]{:S(2)}) copy-start(f32[4096,512]{1,0:T(8,128)S(1)} %fusion.25) | copy-start | bytes 25165828
  104.5 4.1 %copy-start.5 = (s32[1,64]{1,0:T(1,128)S(1)}, s32[1,64]{1,0:T(1,128)}, u32[]{:S(2)}) copy-start(s32[1,64]{1,0:T(1,128)} %param.13) | copy-start | bytes 772
  110.6 15.9 %all-to-all-start = ((f32[64,1,1]{2,1,0:T(1,128)}), f32[64,1,1]{2,1,0:T(1,128)S(1)}, u32[]{:S(2)}, u32[]{:S(2)}) async-start(f32[64,1,1]{2,1,0:T(1,128)} %broadcast_in_dim.2), calls=%async_computation | async-start | bytes 65536 | tf_op jit(solution)/shard_map/all_to_all | solution.py:16
  135.4 1.6 copy-start.2
  135.4 1.8 copy-start.4
  153.2 75.8 %all-to-all-start.3 = ((bf16[2,64,32,512]{3,2,0,1:T(8,128)(2,1)}), bf16[2,64,32,512]{3,2,0,1:T(8,128)(2,1)}, u32[]{:S(2)}, u32[]{:S(2)}) async-start(bf16[2,64,32,512]{3,2,0,1:T(8,128)(2,1)} %copy.23), calls=%async_computation.3 | async-start | bytes 8388608 | tf_op jit(solution)/shard_map/all_to_all | solution.py:96
  238.7 23.4 %copy-start.6 = (s32[1,64]{1,0:T(1,128)S(1)}, s32[1,64]{1,0:T(1,128)}, u32[]{:S(2)}) copy-start(s32[1,64]{1,0:T(1,128)} %param.10) | copy-start | bytes 772
  269.2 8.3 %copy-start.1 = (bf16[512,512]{1,0:T(8,128)(2,1)S(1)}, bf16[512,512]{1,0:T(8,128)(2,1)}, u32[]{:S(2)}) copy-start(bf16[512,512]{1,0:T(8,128)(2,1)} %param.14) | copy-start | bytes 1572868
Sparse Core Ops, SparseCore 0:
  108.7 15.7 all-gather.1
where the time goes:
time: 290 us; the launch traced here: 285 us
  blocking collectives  126 us (43%)
  local copies, waits for them, and re-layouts  49.6 us (17%)
  matrix products  40 us (14%)
  starting transfers between devices  26.5 us (9%)
  between operations  17.4 us (6%)
  other arithmetic  16.2 us (6%)
  waiting for transfers between devices  9.8 us (3%)
    psum x4, blocking collectives, one_axis_at_a_time(): value = lax.psum(value, axis)  67.5 us
    all_to_all x1, blocking collectives, per_device(): lax.all_to_all(owner_interp, GRID, split_axis=1, concat_axis=1, tiled=True)  58.4 us
    convert_element_type x1, local copies, waits for them, and re-layouts, per_device(): returned = jnp.einsum('dkp,mdkc->mdpc', owner_weight, owner_grad, preferr...  23.4 us
    all_to_all x1, starting transfers between devices, per_device(): lax.all_to_all(norm_weight, GRID, split_axis=0, concat_axis=0, tiled=True)  12 us
    gather x1, local copies, waits for them, and re-layouts, per_device(): picked = local_blocks[:, picked_ids]  9.76 us
    dot_general x1, matrix products, per_device(): jnp.einsum('dkp,mdkc->mdpc', owner_weight, owner_grad, preferred_element_...  9.75 us
    dot_general x1, matrix products, per_device(): jnp.einsum('rh,ch->rc', grad_act, w_in, preferred_element_type=jnp.float32)  8.61 us
    transpose x1, local copies, waits for them, and re-layouts, per_device(): jnp.einsum('mdpc,db->mbpc', returned, block_onehot, preferred_element_typ...  8.25 us
  transfers between devices with their start and end apart: 4, of which 2 were waited for; matrix products, arithmetic and copies ran while one was open for 5% of the time, Pallas kernels for 0%

commit v1 on v0

v1 whole, which is shorter than its diff:
```python
import functools

import jax
import jax.numpy as jnp
from jax import lax
from jax.experimental import pallas as pl
from jax.experimental.pallas import tpu as pltpu
from jax.sharding import Mesh
from jax.sharding import PartitionSpec as P

GRID = ("grid_0", "grid_1", "grid_2")
SOFTEN = 0.1
GROUP = 8
PARTS = 2


def forward_kernel(picks, latent, weight, w_in, b_in, w_out, b_out, *refs, first):
    predicted, slope, norm, rows = refs[-4:]
    members, _, width = latent.shape
    group, slots, block = weight.shape
    step = pl.program_id(0)
    raw = weight[...].astype(jnp.float32)
    norm[...] = (raw / jnp.sum(raw, axis=2, keepdims=True)).astype(jnp.bfloat16)
    for d in range(group):
        start = pl.multiple_of(picks[first + step * group + d] * block, block)
        for m in range(members):
            rows[m, d] = jnp.dot(
                norm[d],
                latent[m, pl.ds(start, block), :],
                preferred_element_type=jnp.float32,
            ).astype(jnp.bfloat16)
    for m in range(members):
        flat = rows[m].reshape(group * slots, width)
        pre_act = jnp.dot(flat, w_in[...], preferred_element_type=jnp.float32) + b_in[...]
        gate = 0.5 + 0.5 * jnp.tanh(0.5 * pre_act)
        active = pre_act * gate
        slope[m] = (gate + active * (1.0 - gate)).reshape(group, slots, -1)
        out = jnp.dot(
            active.astype(jnp.bfloat16), w_out[...], preferred_element_type=jnp.float32
        )
        predicted[m] = (out + b_out[...]).reshape(group, slots, -1)


def score_kernel(own, other, payload, info, *refs, members_all, scale):
    grad, loss = refs[-2:]
    members, group, slots, channels = own.shape
    step = pl.program_id(0)
    target = payload[:, :slots, :]
    count = payload[:, slots : slots + 1, :]
    slot = lax.broadcasted_iota(jnp.int32, (group, slots, channels), 1).astype(jnp.float32)
    live = (slot < count).astype(jnp.float32)
    live_total = jnp.sum(info[:, 1:2, :], axis=0)
    factor = live * (scale / live_total)[None]

    def soft(value):
        square = value * value + SOFTEN * SOFTEN
        inverse = lax.rsqrt(square)
        return square * inverse, value * inverse

    mine = [own[i] for i in range(members)]
    theirs = [other[i] for i in range(members)]
    own_obs = [soft(v - target) for v in mine]
    other_obs = [soft(v - target) for v in theirs]
    own_pair = soft(mine[0] - mine[1])
    other_pair = soft(theirs[0] - theirs[1])
    cross = [[soft(a - b) for b in theirs] for a in mine]
    obs_sum = (own_obs[0][0] + own_obs[1][0]) + (other_obs[0][0] + other_obs[1][0])
    pair_sum = (own_pair[0] + other_pair[0]) + (
        (cross[0][0][0] + cross[1][1][0]) + (cross[0][1][0] + cross[1][0][0])
    )
    per_obs = obs_sum / members_all - (2.0 * pair_sum + members_all * SOFTEN) / (
        2.0 * members_all * (members_all - 1)
    )
    part = jnp.sum(jnp.sum(per_obs * live, axis=0), axis=0, keepdims=True)

    @pl.when(step == 0)
    def _():
        loss[...] = jnp.zeros_like(loss)

    loss[...] += part
    pair_scale = 1.0 / (members_all * (members_all - 1.0))
    slope_0 = own_pair[1] + cross[0][0][1] + cross[0][1][1]
    slope_1 = cross[1][0][1] + cross[1][1][1] - own_pair[1]
    for i, slope in enumerate((slope_0, slope_1)):
        grad[i] = (factor * (own_obs[i][1] / members_all - slope * pair_scale)).astype(
            jnp.bfloat16
        )


def backward_kernel(picks, grad, slope, norm, w_in, w_out, out, rows):
    members, group, slots, channels = grad.shape
    block = norm.shape[2]
    width = out.shape[2]
    step = pl.program_id(0)

    @pl.when(step == 0)
    def _():
        out[...] = jnp.zeros_like(out)

    for m in range(members):
        flat = grad[m].reshape(group * slots, channels)
        grad_hidden = lax.dot_general(
            flat, w_out[...], (((1,), (1,)), ((), ())), preferred_element_type=jnp.float32
        )
        grad_act = (grad_hidden * slope[m].reshape(group * slots, -1)).astype(jnp.bfloat16)
        grad_interp = lax.dot_general(
            grad_act, w_in[...], (((1,), (1,)), ((), ())), preferred_element_type=jnp.float32
        )
        rows[m] = grad_interp.astype(jnp.bfloat16).reshape(group, slots, width)
    for d in range(group):
        start = pl.multiple_of(picks[step * group + d] * block, block)
        for m in range(members):
            part = lax.dot_general(
                norm[d],
                rows[m, d],
                (((0,), (0,)), ((), ())),
                preferred_element_type=jnp.float32,
            )
            out[m, pl.ds(start, block), :] += part


def whole(shape):
    return pl.BlockSpec(shape, lambda i, *_: (0,) * len(shape))


def forward_call(first, count, picks, latent, weight, w_in, b_in, w_out, b_out, kept):
    members, points, width = latent.shape
    peers, slots, block = weight.shape
    inner, channels = w_out.shape
    start = first // GROUP
    rows = members * count * slots
    return pl.pallas_call(
        functools.partial(forward_kernel, first=first),
        grid_spec=pltpu.PrefetchScalarGridSpec(
            num_scalar_prefetch=1,
            grid=(count // GROUP,),
            in_specs=[
                whole(latent.shape),
                pl.BlockSpec((GROUP, slots, block), lambda i, *_: (start + i, 0, 0)),
                whole(w_in.shape),
                whole(b_in.shape),
                whole(w_out.shape),
                whole(b_out.shape),
            ]
            + [pl.BlockSpec(memory_space=pl.ANY)] * len(kept),
            out_specs=[
                pl.BlockSpec((members, GROUP, slots, channels), lambda i, *_: (0, i, 0, 0)),
                pl.BlockSpec((members, GROUP, slots, inner), lambda i, *_: (0, start + i, 0, 0)),
                pl.BlockSpec((GROUP, slots, block), lambda i, *_: (start + i, 0, 0)),
            ],
            scratch_shapes=[pltpu.VMEM((members, GROUP, slots, width), jnp.bfloat16)],
        ),
        out_shape=[
            jax.ShapeDtypeStruct((members, count, slots, channels), jnp.float32),
            jax.ShapeDtypeStruct((members, peers, slots, inner), jnp.float32),
            jax.ShapeDtypeStruct((peers, slots, block), jnp.bfloat16),
        ],
        input_output_aliases={7 + i: 1 + i for i in range(len(kept))},
        cost_estimate=pl.CostEstimate(
            flops=2 * rows * (block * width + width * inner + inner * channels),
            bytes_accessed=latent.size * 2 + rows * (inner + channels) * 4,
            transcendentals=rows * inner,
        ),
        name="forward",
    )(picks, latent, weight, w_in, b_in, w_out, b_out, *kept)


def score_call(first, own, other, payload, members_all, scale, kept):
    members, count, slots, channels = own.shape
    start = first // GROUP
    rows = members * count * slots
    block = lambda: pl.BlockSpec((members, GROUP, slots, channels), lambda i: (0, i, 0, 0))
    return pl.pallas_call(
        functools.partial(score_kernel, members_all=members_all, scale=scale),
        grid=(count // GROUP,),
        in_specs=[
            block(),
            block(),
            pl.BlockSpec((GROUP, slots + 8, channels), lambda i: (start + i, 0, 0)),
            pl.BlockSpec((payload.shape[0], 8, channels), lambda i: (0, slots // 8, 0)),
        ]
        + [pl.BlockSpec(memory_space=pl.ANY)] * len(kept),
        out_specs=[
            pl.BlockSpec((members, GROUP, slots, channels), lambda i: (0, start + i, 0, 0)),
            pl.BlockSpec((1, channels), lambda i: (0, 0)),
        ],
        out_shape=[
            jax.ShapeDtypeStruct((members, payload.shape[0], slots, channels), jnp.bfloat16),
            jax.ShapeDtypeStruct((1, channels), jnp.float32),
        ],
        input_output_aliases={4 + i: i for i in range(len(kept))},
        cost_estimate=pl.CostEstimate(
            flops=rows * channels * 40,
            bytes_accessed=rows * channels * 12,
            transcendentals=rows * channels * 5,
        ),
        name="score",
    )(own, other, payload, payload, *kept)


def backward_call(picks, grad, slope, norm, w_in, w_out, points):
    members, count, slots, channels = grad.shape
    width, inner = w_in.shape
    block = norm.shape[2]
    rows = members * count * slots
    return pl.pallas_call(
        backward_kernel,
        grid_spec=pltpu.PrefetchScalarGridSpec(
            num_scalar_prefetch=1,
            grid=(count // GROUP,),
            in_specs=[
                pl.BlockSpec((members, GROUP, slots, channels), lambda i, *_: (0, i, 0, 0)),
                pl.BlockSpec((members, GROUP, slots, inner), lambda i, *_: (0, i, 0, 0)),
                pl.BlockSpec((GROUP, slots, block), lambda i, *_: (i, 0, 0)),
                whole(w_in.shape),
                whole(w_out.shape),
            ],
            out_specs=whole((members, points, width)),
            scratch_shapes=[pltpu.VMEM((members, GROUP, slots, width), jnp.bfloat16)],
        ),
        out_shape=jax.ShapeDtypeStruct((members, points, width), jnp.float32),
        cost_estimate=pl.CostEstimate(
            flops=2 * rows * (block * width + width * inner + inner * channels),
            bytes_accessed=members * points * width * 4 + rows * (inner * 4 + channels * 2),
            transcendentals=0,
        ),
        name="backward",
    )(picks, grad, slope, norm, w_in, w_out)


def swap_members(value):
    return lax.ppermute(value, "member", [(0, 1), (1, 0)])


def to_owners(value):
    return lax.all_to_all(value, GRID, split_axis=0, concat_axis=0, tiled=True)


def per_device(latent, block_pick, obs_weight, obs_value, obs_count, w_in, b_in, w_out, b_out):
    members, points, _ = latent.shape
    peers = lax.axis_size(GRID)
    slots, channels = obs_value.shape[2:]
    members_all = members * lax.axis_size("member")
    picks = block_pick[0]
    counts = obs_count[0]
    weight = to_owners(obs_weight[0])
    live_here = jnp.sum(jnp.minimum(counts, slots)).astype(jnp.float32)
    info = jnp.stack(
        [
            jnp.broadcast_to(counts.astype(jnp.float32)[:, None], (peers, channels)),
            jnp.broadcast_to(live_here, (peers, channels)),
        ],
        axis=1,
    )
    info = jnp.pad(info, ((0, 0), (0, 6), (0, 0)))
    payload = to_owners(jnp.concatenate([obs_value[0], info], axis=1))
    count = peers // PARTS
    b_in = b_in[None]
    b_out = b_out[None]
    kept = ()
    predictions = []
    for part in range(PARTS):
        own, *kept = forward_call(
            part * count, count, picks, latent, weight, w_in, b_in, w_out, b_out, kept
        )
        predictions.append((own, swap_members(own)))
    slope, norm = kept
    scale = float(peers * peers * slots)
    grads = ()
    loss_part = 0.0
    for part, (own, other) in enumerate(predictions):
        *grads, loss = score_call(
            part * count, own, other, payload, members_all, scale, grads
        )
        loss_part += jnp.sum(loss)
    loss_all = to_owners(jnp.broadcast_to(loss_part, (peers, 1, 1)))
    live_total = jnp.sum(payload[:, slots + 1, 0])
    loss_value = jnp.sum(loss_all) / (channels * live_total)
    latent_grad = backward_call(picks, grads[0], slope, norm, w_in, w_out, points)
    return latent_grad, loss_value


def solution(mesh):
    split = Mesh(
        mesh.devices.reshape(mesh.shape["member"], 4, 4, 4),
        ("member", "grid_0", "grid_1", "grid_2"),
    )
    return jax.shard_map(
        per_device,
        mesh=split,
        in_specs=(
            P("member", GRID, None),
            P(GRID, None),
            P(GRID, None, None, None),
            P(GRID, None, None, None),
            P(GRID, None),
            P(),
            P(),
            P(),
            P(),
        ),
        out_specs=(P("member", GRID, None), P()),
        check_vma=False,
    )
```

time: 290 us -> 98.7 us (0.34); the launches traced: 285 us -> 98 us
  blocking collectives: 126 us -> 0 us
  local copies, waits for them, and re-layouts: 49.6 us -> 3.48 us
  Pallas kernels: 0 us -> 45.7 us
  matrix products: 40 us -> 0 us
  between operations: 17.4 us -> 5.12 us
  other arithmetic: 16.2 us -> 5.81 us
    psum x4 -> x0, blocking collectives: 67.5 us -> none  [one_axis_at_a_time(): value = lax.psum(value, axis)]
    all_to_all x1 -> x0, blocking collectives: 58.4 us -> none  [per_device(): lax.all_to_all(owner_interp, GRID, split_axis=1, concat_axis=1, tiled=True)]
    pallas_call x0 -> x5, Pallas kernels: none -> 45.7 us  [the longest x2 19.1 us: forward_call(): pl.pallas_call(functools.partial(forward_kernel, first=first), grid_spec=...]
    dot_general x6 -> x0, matrix products: 40 us -> none  [the longest x1 9.75 us: per_device(): jnp.einsum('dkp,mdkc->mdpc', owner_weight, owner_grad, preferred_element_...]
    convert_element_type x1 -> x0, local copies, waits for them, and re-layouts: 23.4 us -> none  [per_device(): returned = jnp.einsum('dkp,mdkc->mdpc', owner_weight, owner_grad, preferr...]
    gather x1 -> x0, local copies, waits for them, and re-layouts: 9.76 us -> none  [per_device(): picked = local_blocks[:, picked_ids]]
    transpose x1 -> x0, local copies, waits for them, and re-layouts: 8.25 us -> none  [per_device(): jnp.einsum('mdpc,db->mbpc', returned, block_onehot, preferred_element_typ...]
    reduce_sum x5, other arithmetic: 12.7 us -> 4.63 us  [the longest x2 1.78 us: per_device(): loss_part += jnp.sum(loss)]
  transfers between devices with their start and end apart: 4 -> 5, of which waited for: 2 -> 1; matrix products, arithmetic and copies ran while one was open for 5% -> 4% of each run, Pallas kernels for 0% -> 42%
where the time goes in v1:
time: 98.7 us; the launch traced here: 98 us
  Pallas kernels  45.7 us (46%)
  starting transfers between devices  29 us (29%)
  waiting for transfers between devices  8.83 us (9%)
  other arithmetic  5.81 us (6%)
  between operations  5.12 us (5%)
  local copies, waits for them, and re-layouts  3.48 us (4%)
    all_to_all x3, starting transfers between devices, to_owners(): return lax.all_to_all(value, GRID, split_axis=0, concat_axis=0, tiled=True)  26.8 us
    pallas_call x2, Pallas kernels, forward_call(): pl.pallas_call(functools.partial(forward_kernel, first=first), grid_spec=...  19.1 us
    pallas_call x1, Pallas kernels, backward_call(): pl.pallas_call(backward_kernel, grid_spec=pltpu.PrefetchScalarGridSpec(nu...  16.9 us
    pallas_call x2, Pallas kernels, score_call(): pl.pallas_call(functools.partial(score_kernel, members_all=members_all, s...  9.69 us
    all_to_all x3, waiting for transfers between devices, to_owners(): return lax.all_to_all(value, GRID, split_axis=0, concat_axis=0, tiled=True)  8.83 us
    unnamed x12, local copies, waits for them, and re-layouts  2.74 us
    ppermute x2, starting transfers between devices, swap_members(): return lax.ppermute(value, 'member', [(0, 1), (1, 0)])  2.22 us
  transfers between devices with their start and end apart: 5, of which 1 were waited for; matrix products, arithmetic and copies ran while one was open for 4% of the time, Pallas kernels for 42%

profile of v1, /device:TPU:1, one launch (start us, length us, event | category | flops | bytes accessed | tf_op | source)
XLA Modules:
  0.0 98.0 jit_solution(706069796246132868)
XLA Ops:
  0.6 0.0 copy-start.2
  0.6 12.1 %all-to-all-start = ((bf16[64,32,128]{2,1,0:T(8,128)(2,1)}), bf16[64,32,128]{2,1,0:T(8,128)(2,1)S(1)}, u32[]{:S(2)}, u32[]{:S(2)}) async-start(bf16[64,32,128]{2,1,0:T(8,128)(2,1)} %bitcast.8), calls=%async_computation | async-start | bytes 1048576 | tf_op jit(solution)/shard_map/all_to_all | solution.py:236
  12.7 1.4 %minimum_reduce_fusion = (s32[]{:T(128)}, f32[64]{0:T(128)S(1)}) fusion(s32[1,64]{1,0:T(1,128)} %param.13), kind=kLoop, calls=%fused_computation.4 | loop fusion | flops 191 | bytes 516 | tf_op jit(solution)/shard_map/reduce_sum | solution.py:247
  14.8 0.1 stack_broadcast_in_dim.2
  14.9 0.0 copy-done.2
  14.9 1.2 %pad_maximum_fusion = f32[64,40,128]{2,1,0:T(8,128)} fusion(f32[64,8,128]{2,1,0:T(8,128)S(1)} %pad_select_fusion, f32[64,32,128]{2,1,0:T(8,128)S(1)} %bitcast.7), kind=kLoop, calls=%fused_computation | loop fusion | flops 327680 | bytes 2621440 | tf_op jit(solution)/shard_map/concatenate | solution.py:256
  16.1 8.8 %all-to-all-done.weight = bf16[64,32,128]{2,1,0:T(8,128)(2,1)S(1)} async-done(((bf16[64,32,128]{2,1,0:T(8,128)(2,1)}), bf16[64,32,128]{2,1,0:T(8,128)(2,1)S(1)}, u32[]{:S(2)}, u32[]{:S(2)}) %all-to-all-start) | async-done | bytes 524320 | tf_op jit(solution)/shard_map/all_to_all | solution.py:236
  24.9 0.0 copy-start.1
  24.9 0.8 copy-done.1
  25.7 4.7 %all-to-all-start.1 = ((f32[64,40,128]{2,1,0:T(8,128)}), f32[64,40,128]{2,1,0:T(8,128)S(1)}, u32[]{:S(2)}, u32[]{:S(2)}) async-start(f32[64,40,128]{2,1,0:T(8,128)} %pad_maximum_fusion), calls=%async_computation.1 | async-start | bytes 2621440 | tf_op jit(solution)/shard_map/all_to_all | solution.py:236
  30.4 9.5 %forward.2 = (f32[2,32,32,128]{3,2,1,0:T(8,128)}, f32[2,64,32,512]{3,2,1,0:T(8,128)}, bf16[64,32,128]{2,1,0:T(8,128)(2,1)}) custom-call(s32[64]{0:T(128)} %bitcast.9, bf16[2,2048,512]{2,1,0:T(8,128)(2,1)} %latent.3, bf16[64,32,128]{2,1,0:T(8,128)(2,1)} %copy-done.1, bf16[512,512]{1,0:T(8,128)(2,1)} %w_in.5, f32[1,512]{1,0:T(1,128)} %bitcast.12, ...), custom_call_target="tpu_custom_call" | custom-call | flops 1610612736 | bytes 9437184 | tf_op jit(solution)/shard_map/forward/pallas_call | solution.py:132
  39.9 2.2 %collective-permute-start.1 = (f32[2,32,32,128]{3,2,1,0:T(8,128)}, f32[2,32,32,128]{3,2,1,0:T(8,128)S(1)}, u32[]{:S(2)}, u32[]{:S(2)}) collective-permute-start(f32[2,32,32,128]{3,2,1,0:T(8,128)} %get-tuple-element.15.own), channel_id=1, source_target_pairs={{0,64},{64,0},{1,65},{65,1},{2,66},{66,2},{3,67},{67,3},{4,68},{68... | collective-permute-start | bytes 3145736 | tf_op jit(solution)/shard_map/ppermute | solution.py:232
  42.1 9.6 %forward.3 = (f32[2,32,32,128]{3,2,1,0:T(8,128)}, f32[2,64,32,512]{3,2,1,0:T(8,128)}, bf16[64,32,128]{2,1,0:T(8,128)(2,1)}) custom-call(s32[64]{0:T(128)} %bitcast.10, bf16[2,2048,512]{2,1,0:T(8,128)(2,1)} %latent.3, bf16[64,32,128]{2,1,0:T(8,128)(2,1)} %copy-done.1, bf16[512,512]{1,0:T(8,128)(2,1)} %w_in.5, ...), custom_call_target="tpu_custom_call", output_to_operand_aliasing={{1}: (7, {}), {2}: (8, {})} | custom-call | flops 1610612736 | bytes 9437184 | tf_op jit(solution)/shard_map/forward/pallas_call | solution.py:132
  51.8 0.0 collective-permute-start
  51.8 0.0 all-to-all-done.1.payload.info
  51.8 0.0 copy-start
  51.8 0.8 slice_reduce_fusion
  53.2 0.0 collective-permute-done.1.other
  53.3 0.0 copy-done
  53.3 0.0 copy-start.3
  53.3 1.0 copy-done.3
  54.2 4.8 %score.2 = (bf16[2,64,32,128]{3,2,1,0:T(8,128)(2,1)}, f32[1,128]{1,0:T(1,128)}) custom-call(f32[2,32,32,128]{3,2,1,0:T(8,128)} %get-tuple-element.15.own, f32[2,32,32,128]{3,2,1,0:T(8,128)} %copy-done.3, f32[64,40,128]{2,1,0:T(8,128)} %copy-done, f32[64,40,128]{2,1,0:T(8,128)} %copy-done), custom_call_target="tpu_custom_call" | custom-call | flops 10485760 | bytes 3145728 | tf_op jit(solution)/shard_map/score/pallas_call | solution.py:173
  59.1 0.0 collective-permute-done.other
  59.1 0.0 copy-start.4
  59.1 0.9 copy-done.4
  60.0 0.0 copy-start.5
  60.0 4.9 %score.3 = (bf16[2,64,32,128]{3,2,1,0:T(8,128)(2,1)}, f32[1,128]{1,0:T(1,128)}) custom-call(f32[2,32,32,128]{3,2,1,0:T(8,128)} %get-tuple-element.14.own, f32[2,32,32,128]{3,2,1,0:T(8,128)} %copy-done.4, f32[64,40,128]{2,1,0:T(8,128)} %copy-done, f32[64,40,128]{2,1,0:T(8,128)} %copy-done, ...), custom_call_target="tpu_custom_call", output_to_operand_aliasing={{0}: (4, {})} | custom-call | flops 10485760 | bytes 3145728 | tf_op jit(solution)/shard_map/score/pallas_call | solution.py:173
  64.9 1.2 %reduce_sum.47 = f32[]{:T(128)} reduce(f32[1,128]{1,0:T(1,128)} %get-tuple-element.21, f32[]{:T(128)} %constant.3.clone.1), dimensions={0,1}, to_apply=%region_2.3 | reduce | flops 127 | bytes 520 | tf_op jit(solution)/shard_map/reduce_sum | solution.py:275
  66.1 0.0 copy-done.5
  66.1 0.6 reduce_sum.46
  68.0 0.6 broadcast_in_dim.12
  68.6 10.1 %all-to-all-start.2 = ((f32[64,1,1]{2,1,0:T(1,128)}), f32[64,1,1]{2,1,0:T(1,128)S(1)}, u32[]{:S(2)}, u32[]{:S(2)}) async-start(f32[64,1,1]{2,1,0:T(1,128)} %broadcast_in_dim.12), calls=%async_computation.2 | async-start | bytes 65536 | tf_op jit(solution)/shard_map/all_to_all | solution.py:236
  78.7 16.9 %backward.1 = f32[2,2048,512]{2,1,0:T(8,128)} custom-call(s32[64]{0:T(128)} %bitcast.11, bf16[2,64,32,128]{3,2,1,0:T(8,128)(2,1)} %get-tuple-element.17.grad, f32[2,64,32,512]{3,2,1,0:T(8,128)} %get-tuple-element.18.slope, bf16[64,32,128]{2,1,0:T(8,128)(2,1)} %get-tuple-element.19.norm, bf16[512,512]{1,0:T(8,128)(2,1)} %w_in.5, bf16[512,128]{1,0:T(8,128)(2,1)} %w_out.5), custom_call_target="tpu_custom_call" | custom-call | flops 3221225472 | bytes 17825792 | tf_op jit(solution)/shard_map/backward/pallas_call | solution.py:206
  95.6 0.0 all-to-all-done.2
  95.6 0.7 reduce_sum.48
  (1 shorter events, 0.0 us)
Async XLA Ops:
  0.6 14.3 %copy-start.2 = (f32[1,64,32,128]{3,2,1,0:T(8,128)S(1)}, f32[1,64,32,128]{3,2,1,0:T(8,128)}, u32[]{:S(2)}) copy-start(f32[1,64,32,128]{3,2,1,0:T(8,128)} %param.12) | copy-start | bytes 3145732
  0.6 24.3 %all-to-all-start = ((bf16[64,32,128]{2,1,0:T(8,128)(2,1)}), bf16[64,32,128]{2,1,0:T(8,128)(2,1)S(1)}, u32[]{:S(2)}, u32[]{:S(2)}) async-start(bf16[64,32,128]{2,1,0:T(8,128)(2,1)} %bitcast.8), calls=%async_computation | async-start | bytes 1048576 | tf_op jit(solution)/shard_map/all_to_all | solution.py:236
  24.9 0.8 copy-start.1
  25.7 26.1 %all-to-all-start.1 = ((f32[64,40,128]{2,1,0:T(8,128)}), f32[64,40,128]{2,1,0:T(8,128)S(1)}, u32[]{:S(2)}, u32[]{:S(2)}) async-start(f32[64,40,128]{2,1,0:T(8,128)} %pad_maximum_fusion), calls=%async_computation.1 | async-start | bytes 2621440 | tf_op jit(solution)/shard_map/all_to_all | solution.py:236
  39.9 13.3 %collective-permute-start.1 = (f32[2,32,32,128]{3,2,1,0:T(8,128)}, f32[2,32,32,128]{3,2,1,0:T(8,128)S(1)}, u32[]{:S(2)}, u32[]{:S(2)}) collective-permute-start(f32[2,32,32,128]{3,2,1,0:T(8,128)} %get-tuple-element.15.own), channel_id=1, source_target_pairs={{0,64},{64,0},{1,65},{65,1},{2,66},{66,2},{3,67},{67,3},{4,68},{68... | collective-permute-start | bytes 3145736 | tf_op jit(solution)/shard_map/ppermute | solution.py:232
  51.8 7.3 %collective-permute-start = (f32[2,32,32,128]{3,2,1,0:T(8,128)}, f32[2,32,32,128]{3,2,1,0:T(8,128)S(1)}, u32[]{:S(2)}, u32[]{:S(2)}) collective-permute-start(f32[2,32,32,128]{3,2,1,0:T(8,128)} %get-tuple-element.14.own), channel_id=1, source_target_pairs={{0,64},{64,0},{1,65},{65,1},{2,66},{66,2},{3,67},{67,3},{4,68},{68... | collective-permute-start | bytes 3145736 | tf_op jit(solution)/shard_map/ppermute | solution.py:232
  51.8 1.5 %copy-start = (f32[64,40,128]{2,1,0:T(8,128)}, f32[64,40,128]{2,1,0:T(8,128)S(1)}, u32[]{:S(2)}) copy-start(f32[64,40,128]{2,1,0:T(8,128)S(1)} %all-to-all-done.1.payload.info) | copy-start | bytes 3932164
  53.3 1.0 copy-start.3
  59.1 1.0 copy-start.4
  60.0 6.1 %copy-start.5 = (f32[1,128]{1,0:T(1,128)S(1)}, f32[1,128]{1,0:T(1,128)}, u32[]{:S(2)}) copy-start(f32[1,128]{1,0:T(1,128)} %get-tuple-element.20) | copy-start | bytes 1540
  68.6 27.0 %all-to-all-start.2 = ((f32[64,1,1]{2,1,0:T(1,128)}), f32[64,1,1]{2,1,0:T(1,128)S(1)}, u32[]{:S(2)}, u32[]{:S(2)}) async-start(f32[64,1,1]{2,1,0:T(1,128)} %broadcast_in_dim.12), calls=%async_computation.2 | async-start | bytes 65536 | tf_op jit(solution)/shard_map/all_to_all | solution.py:236

commit v2 on v0

v2 whole, which is shorter than its diff:
```python
import functools

import jax
import jax.numpy as jnp
from jax import lax
from jax.experimental import pallas as pl
from jax.experimental.pallas import tpu as pltpu
from jax.sharding import Mesh
from jax.sharding import PartitionSpec as P

GRID = ("grid_0", "grid_1", "grid_2")
SOFTEN = 0.1
PARTS = 2
FORWARD_GROUP = 32
SCORE_GROUP = 8


def forward_kernel(
    picks, latent, weight, w_in, b_in, w_out, b_out, predicted, slope, norm, rows, kept, sems, *, first
):
    members, _, width = latent.shape
    _, slots, block = weight.shape
    count = norm.shape[0]
    group = rows.shape[1]
    copies = []
    for begin in range(0, count, group):
        raw = weight[first + begin : first + begin + group].astype(jnp.float32)
        scaled = (raw / jnp.sum(raw, axis=2, keepdims=True)).astype(jnp.bfloat16)
        norm[begin : begin + group] = scaled
        for d in range(group):
            start = pl.multiple_of(picks[first + begin + d] * block, block)
            for m in range(members):
                rows[m, d] = jnp.dot(
                    scaled[d],
                    latent[m, pl.ds(start, block), :],
                    preferred_element_type=jnp.float32,
                ).astype(jnp.bfloat16)
        for m in range(members):
            flat = rows[m].reshape(group * slots, width)
            pre_act = jnp.dot(flat, w_in[...], preferred_element_type=jnp.float32) + b_in[...]
            gate = 0.5 + 0.5 * jnp.tanh(0.5 * pre_act)
            active = pre_act * gate
            kept[m, begin : begin + group] = (
                (gate + active * (1.0 - gate)).astype(jnp.bfloat16).reshape(group, slots, -1)
            )
            copy = pltpu.make_async_copy(
                kept.at[m, begin : begin + group],
                slope.at[m, begin : begin + group],
                sems.at[len(copies)],
            )
            copy.start()
            copies.append(copy)
            out = jnp.dot(
                active.astype(jnp.bfloat16), w_out[...], preferred_element_type=jnp.float32
            )
            predicted[m, begin : begin + group] = (out + b_out[...]).reshape(group, slots, -1)
    for copy in copies:
        copy.wait()


def score_kernel(own, other, payload, previous, grad, loss, *, first, members_all, scale):
    members, count, slots, channels = own.shape
    live_total = jnp.sum(payload[:, slots + 1, :], axis=0, keepdims=True)
    factor = scale / live_total
    slot = lax.broadcasted_iota(jnp.int32, (SCORE_GROUP, slots, channels), 1).astype(jnp.float32)
    obs_scale = 1.0 / members_all
    pair_scale = 1.0 / (members_all * (members_all - 1.0))

    def soft(value):
        square = value * value + SOFTEN * SOFTEN
        inverse = lax.rsqrt(square)
        return square * inverse, value * inverse

    def body(step, total):
        begin = step * SCORE_GROUP
        here = pl.ds(first + begin, SCORE_GROUP)
        target = payload[here, :slots, :]
        live = (slot < payload[here, slots : slots + 1, :]).astype(jnp.float32)
        mine = [own[i, pl.ds(begin, SCORE_GROUP)] for i in range(members)]
        theirs = [other[i, pl.ds(begin, SCORE_GROUP)] for i in range(members)]
        own_obs = [soft(v - target) for v in mine]
        other_obs = [soft(v - target) for v in theirs]
        own_pair = soft(mine[0] - mine[1])
        other_pair = soft(theirs[0] - theirs[1])
        cross = [[soft(a - b) for b in theirs] for a in mine]
        obs_sum = (own_obs[0][0] + own_obs[1][0]) + (other_obs[0][0] + other_obs[1][0])
        pair_sum = (own_pair[0] + other_pair[0]) + (
            (cross[0][0][0] + cross[1][1][0]) + (cross[0][1][0] + cross[1][0][0])
        )
        per_obs = obs_sum * obs_scale - (pair_sum + members_all * SOFTEN * 0.5) * pair_scale
        slope_0 = own_pair[1] + cross[0][0][1] + cross[0][1][1]
        slope_1 = cross[1][0][1] + cross[1][1][1] - own_pair[1]
        size = live * factor[None]
        for i, slope in enumerate((slope_0, slope_1)):
            grad[i, pl.ds(begin, SCORE_GROUP)] = (
                size * (own_obs[i][1] * obs_scale - slope * pair_scale)
            ).astype(jnp.bfloat16)
        return total + jnp.sum((per_obs * live).reshape(-1, 8, channels), axis=0)

    total = lax.fori_loop(0, count // SCORE_GROUP, body, jnp.zeros((8, channels), jnp.float32))
    total = jnp.sum(total, axis=0, keepdims=True)
    if len(loss.shape) == 2:
        loss[...] = previous[...] + total
    else:
        loss[...] = jnp.broadcast_to((previous[...] + total)[None], loss.shape)


def backward_kernel(*refs):
    picks, w_in, w_out = refs[:3]
    grads = refs[3 : 3 + PARTS]
    slopes = refs[3 + PARTS : 3 + 2 * PARTS]
    norms = refs[3 + 2 * PARTS : 3 + 3 * PARTS]
    out, rows, total, grad, slope, norm, out_sem, grad_sem, slope_sem, norm_sem = refs[
        3 + 3 * PARTS :
    ]
    members, count, slots, channels = grads[0].shape
    block = norms[0].shape[2]
    width = total.shape[2]

    def fetch_grad(m, part, ref):
        return pltpu.make_async_copy(
            ref.at[m], grad.at[m * PARTS + part], grad_sem.at[m * PARTS + part]
        )

    def fetch_slope(m, part, ref):
        return pltpu.make_async_copy(
            ref.at[m], slope.at[m * PARTS + part], slope_sem.at[m * PARTS + part]
        )

    def fetch_norm(part, ref):
        return pltpu.make_async_copy(ref, norm.at[part], norm_sem.at[part])

    for m in range(members):
        for part in range(PARTS):
            fetch_grad(m, part, grads[part]).start()
            fetch_slope(m, part, slopes[part]).start()
            if m == 0:
                fetch_norm(part, norms[part]).start()
    total[...] = jnp.zeros(total.shape, total.dtype)
    for part in range(PARTS):
        fetch_norm(part, norms[part]).wait()

    def body(step, carry):
        m = step // PARTS
        part = step % PARTS
        fetch_grad(m, part, grads[0]).wait()
        fetch_slope(m, part, slopes[0]).wait()
        grad_hidden = lax.dot_general(
            grad[step].reshape(count * slots, channels),
            w_out[...],
            (((1,), (1,)), ((), ())),
            preferred_element_type=jnp.float32,
        )
        grad_act = grad_hidden * slope[step].reshape(count * slots, -1).astype(jnp.float32)
        grad_interp = lax.dot_general(
            grad_act.astype(jnp.bfloat16),
            w_in[...],
            (((1,), (1,)), ((), ())),
            preferred_element_type=jnp.float32,
        )
        rows[...] = grad_interp.astype(jnp.bfloat16).reshape(count, slots, width)
        for d in range(count):
            start = pl.multiple_of(picks[part * count + d] * block, block)
            total[m, pl.ds(start, block), :] += lax.dot_general(
                norm[part, d],
                rows[d],
                (((0,), (0,)), ((), ())),
                preferred_element_type=jnp.float32,
            )

        @pl.when(part == PARTS - 1)
        def _():
            pltpu.make_async_copy(total.at[m], out.at[m], out_sem.at[m]).start()

        return carry

    lax.fori_loop(0, members * PARTS, body, 0)
    for m in range(members):
        pltpu.make_async_copy(total.at[m], out.at[m], out_sem.at[m]).wait()


def vmem(count):
    return [pl.BlockSpec(memory_space=pltpu.VMEM)] * count


def hbm(count):
    return [pl.BlockSpec(memory_space=pltpu.HBM)] * count


def smem():
    return [pl.BlockSpec(memory_space=pltpu.SMEM)]


def forward_call(first, count, picks, latent, weight, w_in, b_in, w_out, b_out):
    members, points, width = latent.shape
    _, slots, block = weight.shape
    inner, channels = w_out.shape
    rows = members * count * slots
    return pl.pallas_call(
        functools.partial(forward_kernel, first=first),
        in_specs=smem() + vmem(6),
        out_specs=vmem(1) + hbm(1) + vmem(1),
        scratch_shapes=[
            pltpu.VMEM((members, FORWARD_GROUP, slots, width), jnp.bfloat16),
            pltpu.VMEM((members, count, slots, inner), jnp.bfloat16),
            pltpu.SemaphoreType.DMA((members * count // FORWARD_GROUP,)),
        ],
        out_shape=[
            jax.ShapeDtypeStruct((members, count, slots, channels), jnp.float32),
            jax.ShapeDtypeStruct((members, count, slots, inner), jnp.bfloat16),
            jax.ShapeDtypeStruct((count, slots, block), jnp.bfloat16),
        ],
        compiler_params=pltpu.CompilerParams(vmem_limit_bytes=16 << 20),
        cost_estimate=pl.CostEstimate(
            flops=2 * rows * (block * width + width * inner + inner * channels),
            bytes_accessed=latent.size * 2 + rows * (inner + channels) * 4,
            transcendentals=rows * inner,
        ),
        name="forward",
    )(picks, latent, weight, w_in, b_in, w_out, b_out)


def score_call(first, own, other, payload, previous, loss_shape, members_all, scale):
    members, count, slots, channels = own.shape
    rows = members * count * slots
    return pl.pallas_call(
        functools.partial(score_kernel, first=first, members_all=members_all, scale=scale),
        in_specs=vmem(4),
        out_specs=vmem(2),
        out_shape=[
            jax.ShapeDtypeStruct(own.shape, jnp.bfloat16),
            jax.ShapeDtypeStruct(loss_shape, jnp.float32),
        ],
        compiler_params=pltpu.CompilerParams(vmem_limit_bytes=8 << 20),
        cost_estimate=pl.CostEstimate(
            flops=rows * channels * 40,
            bytes_accessed=rows * channels * 12,
            transcendentals=rows * channels * 5,
        ),
        name="score",
    )(own, other, payload, previous)


def backward_call(picks, grads, slopes, norms, w_in, w_out, points):
    members, count, slots, channels = grads[0].shape
    width, inner = w_in.shape
    block = norms[0].shape[2]
    rows = members * count * slots * PARTS
    return pl.pallas_call(
        backward_kernel,
        in_specs=smem() + vmem(2) + [pl.BlockSpec(memory_space=pl.ANY)] * (3 * PARTS),
        out_specs=pl.BlockSpec(memory_space=pltpu.HBM),
        scratch_shapes=[
            pltpu.VMEM((count, slots, width), jnp.bfloat16),
            pltpu.VMEM((members, points, width), jnp.float32),
            pltpu.VMEM((members * PARTS, count, slots, channels), jnp.bfloat16),
            pltpu.VMEM((members * PARTS, count, slots, inner), jnp.bfloat16),
            pltpu.VMEM((PARTS, count, slots, block), jnp.bfloat16),
            pltpu.SemaphoreType.DMA((members,)),
            pltpu.SemaphoreType.DMA((members * PARTS,)),
            pltpu.SemaphoreType.DMA((members * PARTS,)),
            pltpu.SemaphoreType.DMA((PARTS,)),
        ],
        out_shape=jax.ShapeDtypeStruct((members, points, width), jnp.float32),
        compiler_params=pltpu.CompilerParams(vmem_limit_bytes=32 << 20),
        cost_estimate=pl.CostEstimate(
            flops=2 * rows * (block * width + width * inner + inner * channels),
            bytes_accessed=members * points * width * 4 + rows * (inner * 4 + channels * 2),
            transcendentals=0,
        ),
        name="backward",
    )(picks, w_in, w_out, *grads, *slopes, *norms)


def swap_members(value):
    return lax.ppermute(value, "member", [(0, 1), (1, 0)])


def to_owners(value):
    return lax.all_to_all(value, GRID, split_axis=0, concat_axis=0, tiled=True)


def per_device(latent, block_pick, obs_weight, obs_value, obs_count, w_in, b_in, w_out, b_out):
    members, points, _ = latent.shape
    peers = lax.axis_size(GRID)
    slots, channels = obs_value.shape[2:]
    members_all = members * lax.axis_size("member")
    picks = block_pick[0]
    counts = obs_count[0]
    weight = to_owners(obs_weight[0])
    live_here = jnp.sum(jnp.minimum(counts, slots)).astype(jnp.float32)
    info = jnp.stack(
        [
            jnp.broadcast_to(counts.astype(jnp.float32)[:, None], (peers, channels)),
            jnp.broadcast_to(live_here, (peers, channels)),
        ],
        axis=1,
    )
    info = jnp.pad(info, ((0, 0), (0, 6), (0, 0)))
    payload = to_owners(jnp.concatenate([obs_value[0], info], axis=1))
    count = peers // PARTS
    b_in = b_in[None]
    b_out = b_out[None]
    parts = []
    for part in range(PARTS):
        own, slope, norm = forward_call(
            part * count, count, picks, latent, weight, w_in, b_in, w_out, b_out
        )
        parts.append((own, swap_members(own), slope, norm))
    scale = float(peers * peers * slots)
    grads = []
    loss = jnp.zeros((1, channels), jnp.float32)
    for part, (own, other, _, _) in enumerate(parts):
        loss_shape = (1, channels) if part + 1 < PARTS else (peers, 8, channels)
        grad, loss = score_call(
            part * count, own, other, payload, loss, loss_shape, members_all, scale
        )
        grads.append(grad)
    loss_all = to_owners(loss)
    live_total = jnp.sum(payload[:, slots + 1, 0])
    loss_value = jnp.sum(loss_all[:, 0, :]) / (channels * live_total)
    latent_grad = backward_call(
        picks, grads, [p[2] for p in parts], [p[3] for p in parts], w_in, w_out, points
    )
    return latent_grad, loss_value


def solution(mesh):
    split = Mesh(
        mesh.devices.reshape(mesh.shape["member"], 4, 4, 4),
        ("member", "grid_0", "grid_1", "grid_2"),
    )
    return jax.shard_map(
        per_device,
        mesh=split,
        in_specs=(
            P("member", GRID, None),
            P(GRID, None),
            P(GRID, None, None, None),
            P(GRID, None, None, None),
            P(GRID, None),
            P(),
            P(),
            P(),
            P(),
        ),
        out_specs=(P("member", GRID, None), P()),
        check_vma=False,
    )
```

time: 290 us -> 93.7 us (0.32); the launches traced: 285 us -> 92.9 us
  blocking collectives: 126 us -> 0 us
  matrix products: 40 us -> 0 us
  local copies, waits for them, and re-layouts: 49.6 us -> 16.8 us
  Pallas kernels: 0 us -> 30.4 us
  between operations: 17.4 us -> 3.94 us
  other arithmetic: 16.2 us -> 3.89 us
    psum x4 -> x0, blocking collectives: 67.5 us -> none  [one_axis_at_a_time(): value = lax.psum(value, axis)]
    all_to_all x1 -> x0, blocking collectives: 58.4 us -> none  [per_device(): lax.all_to_all(owner_interp, GRID, split_axis=1, concat_axis=1, tiled=True)]
    dot_general x6 -> x0, matrix products: 40 us -> none  [the longest x1 9.75 us: per_device(): jnp.einsum('dkp,mdkc->mdpc', owner_weight, owner_grad, preferred_element_...]
    pallas_call x0 -> x5, Pallas kernels: none -> 30.4 us  [the longest x1 12.1 us: backward_call(): pl.pallas_call(backward_kernel, in_specs=smem() + vmem(2) + [pl.BlockSpec...]
    convert_element_type x1 -> x0, local copies, waits for them, and re-layouts: 23.4 us -> none  [per_device(): returned = jnp.einsum('dkp,mdkc->mdpc', owner_weight, owner_grad, preferr...]
    unnamed x20 -> x42, local copies, waits for them, and re-layouts: 1.36 us -> 16.7 us
    reduce_sum x5 -> x3, other arithmetic: 12.7 us -> 2.7 us  [the longest x1 1.37 us: per_device(): live_here = jnp.sum(jnp.minimum(counts, slots)).astype(jnp.float32)]
    gather x1 -> x0, local copies, waits for them, and re-layouts: 9.76 us -> none  [per_device(): picked = local_blocks[:, picked_ids]]
  transfers between devices with their start and end apart: 4 -> 5, of which waited for: 2 -> 1; matrix products, arithmetic and copies ran while one was open for 5% -> 4% of each run, Pallas kernels for 0% -> 29%
where the time goes in v2:
time: 93.7 us; the launch traced here: 92.9 us
  Pallas kernels  30.4 us (32%)
  starting transfers between devices  29 us (31%)
  local copies, waits for them, and re-layouts  16.8 us (18%)
  waiting for transfers between devices  8.81 us (9%)
  between operations  3.94 us (4%)
  other arithmetic  3.89 us (4%)
    all_to_all x3, starting transfers between devices, to_owners(): return lax.all_to_all(value, GRID, split_axis=0, concat_axis=0, tiled=True)  26.8 us
    unnamed x42, local copies, waits for them, and re-layouts  16.7 us
    pallas_call x1, Pallas kernels, backward_call(): pl.pallas_call(backward_kernel, in_specs=smem() + vmem(2) + [pl.BlockSpec...  12.1 us
    pallas_call x2, Pallas kernels, forward_call(): pl.pallas_call(functools.partial(forward_kernel, first=first), in_specs=s...  12 us
    all_to_all x3, waiting for transfers between devices, to_owners(): return lax.all_to_all(value, GRID, split_axis=0, concat_axis=0, tiled=True)  8.8 us
    pallas_call x2, Pallas kernels, score_call(): pl.pallas_call(functools.partial(score_kernel, first=first, members_all=m...  6.36 us
    ppermute x2, starting transfers between devices, swap_members(): return lax.ppermute(value, 'member', [(0, 1), (1, 0)])  2.22 us
  transfers between devices with their start and end apart: 5, of which 1 were waited for; matrix products, arithmetic and copies ran while one was open for 4% of the time, Pallas kernels for 29%

profile of v2, /device:TPU:1, one launch (start us, length us, event | category | flops | bytes accessed | tf_op | source)
XLA Modules:
  0.0 92.9 jit_solution(3330042305983154942)
XLA Ops:
  0.6 0.0 copy-start.20
  0.6 12.1 %all-to-all-start = ((bf16[64,32,128]{2,1,0:T(8,128)(2,1)}), bf16[64,32,128]{2,1,0:T(8,128)(2,1)S(1)}, u32[]{:S(2)}, u32[]{:S(2)}) async-start(bf16[64,32,128]{2,1,0:T(8,128)(2,1)} %bitcast.15), calls=%async_computation | async-start | bytes 1048576 | tf_op jit(solution)/shard_map/all_to_all | solution.py:280
  12.7 1.4 %minimum_reduce_fusion = (s32[]{:T(128)}, f32[64]{0:T(128)S(1)}) fusion(s32[1,64]{1,0:T(1,128)} %param.13), kind=kLoop, calls=%fused_computation.5 | loop fusion | flops 191 | bytes 516 | tf_op jit(solution)/shard_map/reduce_sum | solution.py:291
  14.8 0.1 stack_broadcast_in_dim.2
  14.9 0.0 copy-done.20
  14.9 1.2 %pad_maximum_fusion = f32[64,40,128]{2,1,0:T(8,128)} fusion(f32[64,8,128]{2,1,0:T(8,128)S(1)} %pad_select_fusion, f32[64,32,128]{2,1,0:T(8,128)S(1)} %bitcast.14), kind=kLoop, calls=%fused_computation | loop fusion | flops 327680 | bytes 2621440 | tf_op jit(solution)/shard_map/concatenate | solution.py:300
  16.1 0.0 copy-start.15
  16.1 0.0 copy-start.16
  16.1 0.0 copy-start.18
  16.1 0.0 copy-start.19
  16.1 8.8 %all-to-all-done.weight = bf16[64,32,128]{2,1,0:T(8,128)(2,1)S(1)} async-done(((bf16[64,32,128]{2,1,0:T(8,128)(2,1)}), bf16[64,32,128]{2,1,0:T(8,128)(2,1)S(1)}, u32[]{:S(2)}, u32[]{:S(2)}) %all-to-all-start) | async-done | bytes 524320 | tf_op jit(solution)/shard_map/all_to_all | solution.py:280
  24.9 0.0 copy-start.8
  24.9 0.8 copy-done.8
  25.7 4.7 %all-to-all-start.1 = ((f32[64,40,128]{2,1,0:T(8,128)}), f32[64,40,128]{2,1,0:T(8,128)S(1)}, u32[]{:S(2)}, u32[]{:S(2)}) async-start(f32[64,40,128]{2,1,0:T(8,128)} %pad_maximum_fusion), calls=%async_computation.1 | async-start | bytes 2621440 | tf_op jit(solution)/shard_map/all_to_all | solution.py:280
  30.4 0.0 copy-done.15
  30.4 0.0 copy-done.16
  30.4 0.0 copy-done.18
  30.4 0.0 copy-done.19
  30.4 0.0 copy-start.2
  30.4 1.0 %copy-done.2 = bf16[512,512]{1,0:T(8,128)(2,1)S(1)} copy-done((bf16[512,512]{1,0:T(8,128)(2,1)S(1)}, bf16[512,512]{1,0:T(8,128)(2,1)}, u32[]{:S(2)}) %copy-start.2) | copy-done | bytes 524312
  31.5 0.0 copy-start.9
  31.5 1.0 %copy-done.9 = bf16[64,32,128]{2,1,0:T(8,128)(2,1)S(1)} copy-done((bf16[64,32,128]{2,1,0:T(8,128)(2,1)S(1)}, bf16[64,32,128]{2,1,0:T(8,128)(2,1)}, u32[]{:S(2)}) %copy-start.9) | copy-done | bytes 524312
  32.5 0.0 copy-start.17
  32.5 2.2 %copy-done.17 = bf16[2,2048,512]{2,1,0:T(8,128)(2,1)S(1)} copy-done((bf16[2,2048,512]{2,1,0:T(8,128)(2,1)S(1)}, bf16[2,2048,512]{2,1,0:T(8,128)(2,1)}, u32[]{:S(2)}) %copy-start.17) | copy-done | bytes 4194328
  34.7 6.0 %forward.2 = (f32[2,32,32,128]{3,2,1,0:T(8,128)}, bf16[2,32,32,512]{3,2,1,0:T(8,128)(2,1)S(1)}, bf16[32,32,128]{2,1,0:T(8,128)(2,1)S(1)}) custom-call(s32[64]{0:T(128)S(1)} %bitcast.7, bf16[2,2048,512]{2,1,0:T(8,128)(2,1)S(1)} %copy-done.17, bf16[64,32,128]{2,1,0:T(8,128)(2,1)S(1)} %copy-done.9, bf16[512,512]{1,0:T(8,128)(2,1)S(1)} %copy-done.2, ...), custom_call_target="tpu_custom_call" | custom-call | flops 1610612736 | bytes 9437184 | tf_op jit(solution)/shard_map/forward/pallas_call | solution.py:199
  40.7 0.0 copy-start.10
  40.7 0.7 copy-done.10
  41.4 2.2 %collective-permute-start = (f32[2,32,32,128]{3,2,1,0:T(8,128)}, f32[2,32,32,128]{3,2,1,0:T(8,128)}, u32[]{:S(2)}, u32[]{:S(2)}) collective-permute-start(f32[2,32,32,128]{3,2,1,0:T(8,128)} %get-tuple-element.12.own), channel_id=1, source_target_pairs={{0,64},{64,0},{1,65},{65,1},{2,66},{66,2},{3,67},{67,3},{4,68},{68... | collective-permute-start | bytes 3145736 | tf_op jit(solution)/shard_map/ppermute | solution.py:276
  43.6 6.0 %forward.3 = (f32[2,32,32,128]{3,2,1,0:T(8,128)}, bf16[2,32,32,512]{3,2,1,0:T(8,128)(2,1)S(1)}, bf16[32,32,128]{2,1,0:T(8,128)(2,1)S(1)}) custom-call(s32[64]{0:T(128)S(1)} %bitcast.8, bf16[2,2048,512]{2,1,0:T(8,128)(2,1)S(1)} %copy-done.17, bf16[64,32,128]{2,1,0:T(8,128)(2,1)S(1)} %copy-done.9, bf16[512,512]{1,0:T(8,128)(2,1)S(1)} %copy-done.2, ...), custom_call_target="tpu_custom_call" | custom-call | flops 1610612736 | bytes 9437184 | tf_op jit(solution)/shard_map/forward/pallas_call | solution.py:199
  49.6 0.0 copy-start
  49.6 1.3 %copy-done = bf16[2,32,32,512]{3,2,1,0:T(8,128)(2,1)} copy-done((bf16[2,32,32,512]{3,2,1,0:T(8,128)(2,1)}, bf16[2,32,32,512]{3,2,1,0:T(8,128)(2,1)S(1)}, u32[]{:S(2)}) %copy-start) | copy-done | bytes 2097176
  51.0 0.0 copy-start.12
  51.0 0.7 copy-done.12
  51.7 0.0 collective-permute-start.1
  51.7 0.0 all-to-all-done.1.payload
  51.7 0.7 slice_reduce_fusion
  53.0 0.0 collective-permute-done.other
  53.0 3.2 %score.2 = (bf16[2,32,32,128]{3,2,1,0:T(8,128)(2,1)S(1)}, f32[1,128]{1,0:T(1,128)S(1)}) custom-call(f32[2,32,32,128]{3,2,1,0:T(8,128)} %get-tuple-element.12.own, f32[2,32,32,128]{3,2,1,0:T(8,128)} %collective-permute-done.other, f32[64,40,128]{2,1,0:T(8,128)S(1)} %all-to-all-done.1.payload, f32[1,128]{1,0:T(1,128)S(1)} %broadcast_in_dim.12.previous), custom_call_target="tpu_custom_call" | custom-call | flops 10485760 | bytes 3145728 | tf_op jit(solution)/shard_map/score/pallas_call | solution.py:226
  56.2 0.0 copy-start.4
  56.2 0.8 copy-done.4
  57.0 0.0 collective-permute-done.1.other
  57.0 3.2 %score.3 = (bf16[2,32,32,128]{3,2,1,0:T(8,128)(2,1)S(1)}, f32[64,8,128]{2,1,0:T(8,128)S(1)}) custom-call(f32[2,32,32,128]{3,2,1,0:T(8,128)} %get-tuple-element.14.own, f32[2,32,32,128]{3,2,1,0:T(8,128)} %collective-permute-done.1.other, f32[64,40,128]{2,1,0:T(8,128)S(1)} %all-to-all-done.1.payload, f32[1,128]{1,0:T(1,128)S(1)} %get-tuple-element.15.previous), custom_call_target="tpu_custom_call" | custom-call | flops 10485760 | bytes 3145728 | tf_op jit(solution)/shard_map/score/pallas_call | solution.py:226
  60.2 0.0 copy-start.6
  60.2 0.8 copy-done.6
  61.0 0.0 copy-start.14
  61.0 0.7 copy-done.14
  61.7 10.1 %all-to-all-start.2 = ((f32[64,8,128]{2,1,0:T(8,128)}), f32[64,8,128]{2,1,0:T(8,128)S(1)}, u32[]{:S(2)}, u32[]{:S(2)}) async-start(f32[64,8,128]{2,1,0:T(8,128)} %copy-done.14), calls=%async_computation.2 | async-start | bytes 524288 | tf_op jit(solution)/shard_map/all_to_all | solution.py:280
  71.7 0.0 copy-start.1
  71.7 1.6 %copy-done.1 = bf16[2,32,32,512]{3,2,1,0:T(8,128)(2,1)S(1)} copy-done((bf16[2,32,32,512]{3,2,1,0:T(8,128)(2,1)S(1)}, bf16[2,32,32,512]{3,2,1,0:T(8,128)(2,1)}, u32[]{:S(2)}) %copy-start.1) | copy-done | bytes 2097176
  73.3 0.0 copy-start.3
  73.3 1.0 %copy-done.3 = bf16[512,512]{1,0:T(8,128)(2,1)S(1)} copy-done((bf16[512,512]{1,0:T(8,128)(2,1)S(1)}, bf16[512,512]{1,0:T(8,128)(2,1)}, u32[]{:S(2)}) %copy-start.3) | copy-done | bytes 524312
  74.4 0.0 copy-start.5
  74.4 1.0 %copy-done.5 = bf16[2,32,32,128]{3,2,1,0:T(8,128)(2,1)S(1)} copy-done((bf16[2,32,32,128]{3,2,1,0:T(8,128)(2,1)S(1)}, bf16[2,32,32,128]{3,2,1,0:T(8,128)(2,1)}, u32[]{:S(2)}) %copy-start.5) | copy-done | bytes 524312
  75.4 0.0 copy-start.7
  75.4 1.0 %copy-done.7 = bf16[2,32,32,128]{3,2,1,0:T(8,128)(2,1)S(1)} copy-done((bf16[2,32,32,128]{3,2,1,0:T(8,128)(2,1)S(1)}, bf16[2,32,32,128]{3,2,1,0:T(8,128)(2,1)}, u32[]{:S(2)}) %copy-start.7) | copy-done | bytes 524312
  76.4 0.0 copy-start.11
  76.5 0.9 %copy-done.11 = bf16[32,32,128]{2,1,0:T(8,128)(2,1)S(1)} copy-done((bf16[32,32,128]{2,1,0:T(8,128)(2,1)S(1)}, bf16[32,32,128]{2,1,0:T(8,128)(2,1)}, u32[]{:S(2)}) %copy-start.11) | copy-done | bytes 262168
  77.4 0.0 copy-start.13
  77.4 0.9 %copy-done.13 = bf16[32,32,128]{2,1,0:T(8,128)(2,1)S(1)} copy-done((bf16[32,32,128]{2,1,0:T(8,128)(2,1)S(1)}, bf16[32,32,128]{2,1,0:T(8,128)(2,1)}, u32[]{:S(2)}) %copy-start.13) | copy-done | bytes 262168
  78.3 12.1 %backward.1 = f32[2,2048,512]{2,1,0:T(8,128)} custom-call(s32[64]{0:T(128)S(1)} %bitcast.9, bf16[512,512]{1,0:T(8,128)(2,1)S(1)} %copy-done.3, bf16[512,128]{1,0:T(8,128)(2,1)S(1)} %copy-done.15, bf16[2,32,32,128]{3,2,1,0:T(8,128)(2,1)S(1)} %copy-done.5, bf16[2,32,32,128]{3,2,1,0:T(8,128)(2,1)S(1)} %copy-done.7, ...), custom_call_target="tpu_custom_call" | custom-call | flops 3221225472 | bytes 17825792 | tf_op jit(solution)/shard_map/backward/pallas_call | solution.py:249
  90.4 0.0 all-to-all-done.2
  90.4 0.7 slice_reduce_fusion.1
  (2 shorter events, 0.0 us)
Async XLA Ops:
  0.6 14.3 %copy-start.20 = (f32[1,64,32,128]{3,2,1,0:T(8,128)S(1)}, f32[1,64,32,128]{3,2,1,0:T(8,128)}, u32[]{:S(2)}) copy-start(f32[1,64,32,128]{3,2,1,0:T(8,128)} %param.12) | copy-start | bytes 3145732
  0.6 24.3 %all-to-all-start = ((bf16[64,32,128]{2,1,0:T(8,128)(2,1)}), bf16[64,32,128]{2,1,0:T(8,128)(2,1)S(1)}, u32[]{:S(2)}, u32[]{:S(2)}) async-start(bf16[64,32,128]{2,1,0:T(8,128)(2,1)} %bitcast.15), calls=%async_computation | async-start | bytes 1048576 | tf_op jit(solution)/shard_map/all_to_all | solution.py:280
  16.1 14.3 %copy-start.15 = (bf16[512,128]{1,0:T(8,128)(2,1)S(1)}, bf16[512,128]{1,0:T(8,128)(2,1)}, u32[]{:S(2)}) copy-start(bf16[512,128]{1,0:T(8,128)(2,1)} %refs_2_.1) | copy-start | bytes 393220
  16.1 14.3 %copy-start.16 = (s32[1,64]{1,0:T(1,128)S(1)}, s32[1,64]{1,0:T(1,128)}, u32[]{:S(2)}) copy-start(s32[1,64]{1,0:T(1,128)} %param.10) | copy-start | bytes 772
  16.1 14.3 %copy-start.18 = (f32[512]{0:T(512)S(1)}, f32[512]{0:T(512)}, u32[]{:S(2)}) copy-start(f32[512]{0:T(512)} %param.15) | copy-start | bytes 6148
  16.1 14.3 %copy-start.19 = (f32[128]{0:T(128)S(1)}, f32[128]{0:T(128)}, u32[]{:S(2)}) copy-start(f32[128]{0:T(128)} %param.17) | copy-start | bytes 1540
  24.9 0.8 copy-start.8
  25.7 26.0 %all-to-all-start.1 = ((f32[64,40,128]{2,1,0:T(8,128)}), f32[64,40,128]{2,1,0:T(8,128)S(1)}, u32[]{:S(2)}, u32[]{:S(2)}) async-start(f32[64,40,128]{2,1,0:T(8,128)} %pad_maximum_fusion), calls=%async_computation.1 | async-start | bytes 2621440 | tf_op jit(solution)/shard_map/all_to_all | solution.py:280
  30.4 1.0 %copy-start.2 = (bf16[512,512]{1,0:T(8,128)(2,1)S(1)}, bf16[512,512]{1,0:T(8,128)(2,1)}, u32[]{:S(2)}) copy-start(bf16[512,512]{1,0:T(8,128)(2,1)} %refs_1_.1) | copy-start | bytes 1572868
  31.5 1.0 %copy-start.9 = (bf16[64,32,128]{2,1,0:T(8,128)(2,1)S(1)}, bf16[64,32,128]{2,1,0:T(8,128)(2,1)}, u32[]{:S(2)}) copy-start(bf16[64,32,128]{2,1,0:T(8,128)(2,1)} %copy-done.8) | copy-start | bytes 1572868
  32.5 2.2 %copy-start.17 = (bf16[2,2048,512]{2,1,0:T(8,128)(2,1)S(1)}, bf16[2,2048,512]{2,1,0:T(8,128)(2,1)}, u32[]{:S(2)}) copy-start(bf16[2,2048,512]{2,1,0:T(8,128)(2,1)} %latent.3) | copy-start | bytes 12582916
  40.7 0.7 copy-start.10
  41.4 11.6 %collective-permute-start = (f32[2,32,32,128]{3,2,1,0:T(8,128)}, f32[2,32,32,128]{3,2,1,0:T(8,128)}, u32[]{:S(2)}, u32[]{:S(2)}) collective-permute-start(f32[2,32,32,128]{3,2,1,0:T(8,128)} %get-tuple-element.12.own), channel_id=1, source_target_pairs={{0,64},{64,0},{1,65},{65,1},{2,66},{66,2},{3,67},{67,3},{4,68},{68... | collective-permute-start | bytes 3145736 | tf_op jit(solution)/shard_map/ppermute | solution.py:276
  49.6 1.3 %copy-start = (bf16[2,32,32,512]{3,2,1,0:T(8,128)(2,1)}, bf16[2,32,32,512]{3,2,1,0:T(8,128)(2,1)S(1)}, u32[]{:S(2)}) copy-start(bf16[2,32,32,512]{3,2,1,0:T(8,128)(2,1)S(1)} %get-tuple-element.18.refs_6_) | copy-start | bytes 6291460
  51.0 0.7 copy-start.12
  51.7 5.3 %collective-permute-start.1 = (f32[2,32,32,128]{3,2,1,0:T(8,128)}, f32[2,32,32,128]{3,2,1,0:T(8,128)}, u32[]{:S(2)}, u32[]{:S(2)}) collective-permute-start(f32[2,32,32,128]{3,2,1,0:T(8,128)} %get-tuple-element.14.own), channel_id=1, source_target_pairs={{0,64},{64,0},{1,65},{65,1},{2,66},{66,2},{3,67},{67,3},{4,68},{68... | collective-permute-start | bytes 3145736 | tf_op jit(solution)/shard_map/ppermute | solution.py:276
  56.2 0.8 copy-start.4
  60.2 0.8 copy-start.6
  61.0 0.7 copy-start.14
  61.7 28.7 %all-to-all-start.2 = ((f32[64,8,128]{2,1,0:T(8,128)}), f32[64,8,128]{2,1,0:T(8,128)S(1)}, u32[]{:S(2)}, u32[]{:S(2)}) async-start(f32[64,8,128]{2,1,0:T(8,128)} %copy-done.14), calls=%async_computation.2 | async-start | bytes 524288 | tf_op jit(solution)/shard_map/all_to_all | solution.py:280
  71.7 1.6 %copy-start.1 = (bf16[2,32,32,512]{3,2,1,0:T(8,128)(2,1)S(1)}, bf16[2,32,32,512]{3,2,1,0:T(8,128)(2,1)}, u32[]{:S(2)}) copy-start(bf16[2,32,32,512]{3,2,1,0:T(8,128)(2,1)} %copy-done) | copy-start | bytes 6291460
  73.3 1.0 %copy-start.3 = (bf16[512,512]{1,0:T(8,128)(2,1)S(1)}, bf16[512,512]{1,0:T(8,128)(2,1)}, u32[]{:S(2)}) copy-start(bf16[512,512]{1,0:T(8,128)(2,1)} %refs_1_.1) | copy-start | bytes 1572868
  74.4 1.0 %copy-start.5 = (bf16[2,32,32,128]{3,2,1,0:T(8,128)(2,1)S(1)}, bf16[2,32,32,128]{3,2,1,0:T(8,128)(2,1)}, u32[]{:S(2)}) copy-start(bf16[2,32,32,128]{3,2,1,0:T(8,128)(2,1)} %copy-done.4) | copy-start | bytes 1572868
  75.4 1.0 %copy-start.7 = (bf16[2,32,32,128]{3,2,1,0:T(8,128)(2,1)S(1)}, bf16[2,32,32,128]{3,2,1,0:T(8,128)(2,1)}, u32[]{:S(2)}) copy-start(bf16[2,32,32,128]{3,2,1,0:T(8,128)(2,1)} %copy-done.6) | copy-start | bytes 1572868
  76.4 0.9 %copy-start.11 = (bf16[32,32,128]{2,1,0:T(8,128)(2,1)S(1)}, bf16[32,32,128]{2,1,0:T(8,128)(2,1)}, u32[]{:S(2)}) copy-start(bf16[32,32,128]{2,1,0:T(8,128)(2,1)} %copy-done.10) | copy-start | bytes 786436
  77.4 0.9 %copy-start.13 = (bf16[32,32,128]{2,1,0:T(8,128)(2,1)S(1)}, bf16[32,32,128]{2,1,0:T(8,128)(2,1)}, u32[]{:S(2)}) copy-start(bf16[32,32,128]{2,1,0:T(8,128)(2,1)} %copy-done.12) | copy-start | bytes 786436

commit v3 on v2

v3 whole, which is shorter than its diff:
```python
import functools

import jax
import jax.numpy as jnp
from jax import lax
from jax.experimental import pallas as pl
from jax.experimental.pallas import tpu as pltpu
from jax.sharding import Mesh
from jax.sharding import PartitionSpec as P

GRID = ("grid_0", "grid_1", "grid_2")
SOFTEN = 0.1
HALVES = 2
SCORE_GROUP = 8


def forward_kernel(
    picks,
    latent,
    weight,
    w_in,
    b_in,
    w_out,
    b_out,
    predicted,
    slope,
    norm,
    latent_here,
    weight_here,
    w_in_here,
    rows,
    predicted_here,
    slope_here,
    norm_here,
    latent_sem,
    weight_sem,
    w_in_sem,
    predicted_sem,
    slope_sem,
    norm_sem,
):
    members, _, width = latent.shape
    peers, slots, block = weight.shape
    half = peers // HALVES

    def fetch(m):
        return pltpu.make_async_copy(latent.at[m], latent_here.at[m], latent_sem.at[m])

    def put_predicted(step, m, begin):
        return pltpu.make_async_copy(
            predicted_here.at[step], predicted.at[m, pl.ds(begin, half)], predicted_sem.at[step]
        )

    def put_slope(step, m, begin):
        return pltpu.make_async_copy(
            slope_here.at[step], slope.at[m, pl.ds(begin, half)], slope_sem.at[step]
        )

    fetch_weight = pltpu.make_async_copy(weight, weight_here, weight_sem)
    fetch_w_in = pltpu.make_async_copy(w_in, w_in_here, w_in_sem)
    put_norm = pltpu.make_async_copy(norm_here, norm, norm_sem)
    fetch_weight.start()
    fetch(0).start()
    fetch_w_in.start()
    fetch(1).start()
    fetch_weight.wait()
    raw = weight_here[...].astype(jnp.float32)
    norm_here[...] = (raw / jnp.sum(raw, axis=2, keepdims=True)).astype(jnp.bfloat16)
    put_norm.start()
    fetch_w_in.wait()

    def body(step, carry):
        m = step // HALVES
        begin = (step % HALVES) * half

        @pl.when(step % HALVES == 0)
        def _():
            fetch(m).wait()

        for d in range(half):
            start = pl.multiple_of(picks[begin + d] * block, block)
            rows[d] = jnp.dot(
                norm_here[begin + d],
                latent_here[m, pl.ds(start, block), :],
                preferred_element_type=jnp.float32,
            ).astype(jnp.bfloat16)
        flat = rows[...].reshape(half * slots, width)
        pre_act = jnp.dot(flat, w_in_here[...], preferred_element_type=jnp.float32) + b_in[...]
        gate = 0.5 + 0.5 * jnp.tanh(0.5 * pre_act)
        active = pre_act * gate
        slope_here[step] = (
            (gate + active * (1.0 - gate)).astype(jnp.bfloat16).reshape(half, slots, -1)
        )
        put_slope(step, m, begin).start()
        out = jnp.dot(active.astype(jnp.bfloat16), w_out[...], preferred_element_type=jnp.float32)
        predicted_here[step] = (out + b_out[...]).reshape(half, slots, -1)
        put_predicted(step, m, begin).start()
        return carry

    lax.fori_loop(0, members * HALVES, body, 0)
    put_norm.wait()
    for step in range(members * HALVES):
        put_slope(step, step // HALVES, (step % HALVES) * half).wait()
        put_predicted(step, step // HALVES, (step % HALVES) * half).wait()


def score_kernel(
    own,
    other,
    payload,
    grad,
    loss,
    own_here,
    other_here,
    payload_here,
    grad_here,
    own_sem,
    other_sem,
    payload_sem,
    grad_sem,
    *,
    members_all,
    scale,
):
    members, peers, slots, channels = own.shape
    steps = peers // SCORE_GROUP

    def fetch(source, target, sem, step):
        here = pl.ds(step * SCORE_GROUP, SCORE_GROUP)
        return pltpu.make_async_copy(source.at[:, here], target.at[:, here], sem.at[step])

    fetch_payload = pltpu.make_async_copy(payload, payload_here, payload_sem)
    fetch_payload.start()
    for step in range(steps):
        fetch(own, own_here, own_sem, step).start()
        fetch(other, other_here, other_sem, step).start()
    fetch_payload.wait()
    live_total = jnp.sum(payload_here[:, slots + 1, :], axis=0, keepdims=True)
    factor = scale / live_total
    slot = lax.broadcasted_iota(jnp.int32, (SCORE_GROUP, slots, channels), 1).astype(jnp.float32)
    obs_scale = 1.0 / members_all
    pair_scale = 1.0 / (members_all * (members_all - 1.0))

    def soft(value):
        square = value * value + SOFTEN * SOFTEN
        inverse = lax.rsqrt(square)
        return square * inverse, value * inverse

    def body(step, total):
        here = pl.ds(step * SCORE_GROUP, SCORE_GROUP)
        fetch(own, own_here, own_sem, step).wait()
        fetch(other, other_here, other_sem, step).wait()
        target = payload_here[here, :slots, :]
        live = (slot < payload_here[here, slots : slots + 1, :]).astype(jnp.float32)
        mine = [own_here[i, here] for i in range(members)]
        theirs = [other_here[i, here] for i in range(members)]
        own_obs = [soft(v - target) for v in mine]
        other_obs = [soft(v - target) for v in theirs]
        own_pair = soft(mine[0] - mine[1])
        other_pair = soft(theirs[0] - theirs[1])
        cross = [[soft(a - b) for b in theirs] for a in mine]
        obs_sum = (own_obs[0][0] + own_obs[1][0]) + (other_obs[0][0] + other_obs[1][0])
        pair_sum = (own_pair[0] + other_pair[0]) + (
            (cross[0][0][0] + cross[1][1][0]) + (cross[0][1][0] + cross[1][0][0])
        )
        per_obs = obs_sum * obs_scale - (pair_sum + members_all * SOFTEN * 0.5) * pair_scale
        slope_0 = own_pair[1] + cross[0][0][1] + cross[0][1][1]
        slope_1 = cross[1][0][1] + cross[1][1][1] - own_pair[1]
        size = live * factor[None]
        for i, slope in enumerate((slope_0, slope_1)):
            grad_here[i, here] = (
                size * (own_obs[i][1] * obs_scale - slope * pair_scale)
            ).astype(jnp.bfloat16)
        fetch(grad_here, grad, grad_sem, step).start()
        return total + jnp.sum((per_obs * live).reshape(-1, 8, channels), axis=0)

    total = lax.fori_loop(0, steps, body, jnp.zeros((8, channels), jnp.float32))
    total = jnp.sum(total, axis=0, keepdims=True)
    loss[...] = jnp.broadcast_to(total[None], loss.shape)
    for step in range(steps):
        fetch(grad_here, grad, grad_sem, step).wait()


def backward_kernel(
    picks,
    w_in,
    w_out,
    grad,
    slope,
    norm,
    out,
    w_in_here,
    rows,
    total,
    grad_here,
    slope_here,
    norm_here,
    w_in_sem,
    out_sem,
    grad_sem,
    slope_sem,
    norm_sem,
):
    members, peers, slots, channels = grad.shape
    block = norm.shape[2]
    width = total.shape[2]
    half = peers // HALVES

    def fetch_grad(step, m, begin):
        return pltpu.make_async_copy(
            grad.at[m, pl.ds(begin, half)], grad_here.at[step], grad_sem.at[step]
        )

    def fetch_slope(step, m, begin):
        return pltpu.make_async_copy(
            slope.at[m, pl.ds(begin, half)], slope_here.at[step], slope_sem.at[step]
        )

    def put(m):
        return pltpu.make_async_copy(total.at[m], out.at[m], out_sem.at[m])

    fetch_w_in = pltpu.make_async_copy(w_in, w_in_here, w_in_sem)
    fetch_norm = pltpu.make_async_copy(norm, norm_here, norm_sem)
    for step in range(members * HALVES):
        fetch_grad(step, step // HALVES, (step % HALVES) * half).start()
        fetch_slope(step, step // HALVES, (step % HALVES) * half).start()
        if step == 0:
            fetch_w_in.start()
            fetch_norm.start()
    total[...] = jnp.zeros(total.shape, total.dtype)
    fetch_w_in.wait()
    fetch_norm.wait()

    def body(step, carry):
        m = step // HALVES
        begin = (step % HALVES) * half
        fetch_grad(step, m, begin).wait()
        fetch_slope(step, m, begin).wait()
        grad_hidden = lax.dot_general(
            grad_here[step].reshape(half * slots, channels),
            w_out[...],
            (((1,), (1,)), ((), ())),
            preferred_element_type=jnp.float32,
        )
        grad_act = grad_hidden * slope_here[step].reshape(half * slots, -1).astype(jnp.float32)
        grad_interp = lax.dot_general(
            grad_act.astype(jnp.bfloat16),
            w_in_here[...],
            (((1,), (1,)), ((), ())),
            preferred_element_type=jnp.float32,
        )
        rows[...] = grad_interp.astype(jnp.bfloat16).reshape(half, slots, width)
        for d in range(half):
            start = pl.multiple_of(picks[begin + d] * block, block)
            total[m, pl.ds(start, block), :] += lax.dot_general(
                norm_here[begin + d],
                rows[d],
                (((0,), (0,)), ((), ())),
                preferred_element_type=jnp.float32,
            )

        @pl.when(step % HALVES == HALVES - 1)
        def _():
            put(m).start()

        return carry

    lax.fori_loop(0, members * HALVES, body, 0)
    for m in range(members):
        put(m).wait()


def vmem(count):
    return [pl.BlockSpec(memory_space=pltpu.VMEM)] * count


def smem():
    return [pl.BlockSpec(memory_space=pltpu.SMEM)]


def left(count):
    return [pl.BlockSpec(memory_space=pl.ANY)] * count


def dma(*shape):
    return pltpu.SemaphoreType.DMA(shape) if shape else pltpu.SemaphoreType.DMA


def forward_call(picks, latent, weight, w_in, b_in, w_out, b_out):
    members, _, width = latent.shape
    peers, slots, block = weight.shape
    inner, channels = w_out.shape
    rows = members * peers * slots
    steps = members * HALVES
    half = peers // HALVES
    return pl.pallas_call(
        forward_kernel,
        in_specs=smem() + left(3) + vmem(3),
        out_specs=left(3),
        scratch_shapes=[
            pltpu.VMEM(latent.shape, jnp.bfloat16),
            pltpu.VMEM(weight.shape, jnp.bfloat16),
            pltpu.VMEM(w_in.shape, jnp.bfloat16),
            pltpu.VMEM((half, slots, width), jnp.bfloat16),
            pltpu.VMEM((steps, half, slots, channels), jnp.float32),
            pltpu.VMEM((steps, half, slots, inner), jnp.bfloat16),
            pltpu.VMEM(weight.shape, jnp.bfloat16),
            dma(members),
            dma(),
            dma(),
            dma(steps),
            dma(steps),
            dma(),
        ],
        out_shape=[
            jax.ShapeDtypeStruct((members, peers, slots, channels), jnp.float32),
            jax.ShapeDtypeStruct((members, peers, slots, inner), jnp.bfloat16),
            jax.ShapeDtypeStruct(weight.shape, jnp.bfloat16),
        ],
        cost_estimate=pl.CostEstimate(
            flops=2 * rows * (block * width + width * inner + inner * channels),
            bytes_accessed=latent.size * 2 + rows * (inner * 2 + channels * 4),
            transcendentals=rows * inner,
        ),
        name="forward",
    )(picks, latent, weight, w_in, b_in, w_out, b_out)


def score_call(own, other, payload, members_all, scale):
    members, peers, slots, channels = own.shape
    rows = members * peers * slots
    steps = peers // SCORE_GROUP
    return pl.pallas_call(
        functools.partial(score_kernel, members_all=members_all, scale=scale),
        in_specs=left(3),
        out_specs=left(1) + vmem(1),
        out_shape=[
            jax.ShapeDtypeStruct(own.shape, jnp.bfloat16),
            jax.ShapeDtypeStruct((peers, 8, channels), jnp.float32),
        ],
        scratch_shapes=[
            pltpu.VMEM(own.shape, jnp.float32),
            pltpu.VMEM(own.shape, jnp.float32),
            pltpu.VMEM(payload.shape, jnp.float32),
            pltpu.VMEM(own.shape, jnp.bfloat16),
            dma(steps),
            dma(steps),
            dma(),
            dma(steps),
        ],
        cost_estimate=pl.CostEstimate(
            flops=rows * channels * 40,
            bytes_accessed=rows * channels * 12,
            transcendentals=rows * channels * 5,
        ),
        name="score",
    )(own, other, payload)


def backward_call(picks, grad, slope, norm, w_in, w_out, points):
    members, peers, slots, channels = grad.shape
    width, inner = w_in.shape
    block = norm.shape[2]
    rows = members * peers * slots
    steps = members * HALVES
    half = peers // HALVES
    return pl.pallas_call(
        backward_kernel,
        in_specs=smem() + left(1) + vmem(1) + left(3),
        out_specs=pl.BlockSpec(memory_space=pl.ANY),
        scratch_shapes=[
            pltpu.VMEM(w_in.shape, jnp.bfloat16),
            pltpu.VMEM((half, slots, width), jnp.bfloat16),
            pltpu.VMEM((members, points, width), jnp.float32),
            pltpu.VMEM((steps, half, slots, channels), jnp.bfloat16),
            pltpu.VMEM((steps, half, slots, inner), jnp.bfloat16),
            pltpu.VMEM(norm.shape, jnp.bfloat16),
            dma(),
            dma(members),
            dma(steps),
            dma(steps),
            dma(),
        ],
        out_shape=jax.ShapeDtypeStruct((members, points, width), jnp.float32),
        cost_estimate=pl.CostEstimate(
            flops=2 * rows * (block * width + width * inner + inner * channels),
            bytes_accessed=members * points * width * 4 + rows * (inner * 2 + channels * 2),
            transcendentals=0,
        ),
        name="backward",
    )(picks, w_in, w_out, grad, slope, norm)


def swap_members(value):
    return lax.ppermute(value, "member", [(0, 1), (1, 0)])


def to_owners(value):
    return lax.all_to_all(value, GRID, split_axis=0, concat_axis=0, tiled=True)


def device_step(latent, block_pick, obs_weight, obs_value, obs_count, w_in, b_in, w_out, b_out):
    members, points, _ = latent.shape
    peers = lax.axis_size(GRID)
    slots, channels = obs_value.shape[2:]
    members_all = members * lax.axis_size("member")
    picks = block_pick[0]
    counts = obs_count[0]
    weight = to_owners(obs_weight[0])
    live_here = jnp.sum(jnp.minimum(counts, slots)).astype(jnp.float32)
    info = jnp.stack(
        [
            jnp.broadcast_to(counts.astype(jnp.float32)[:, None], (peers, channels)),
            jnp.broadcast_to(live_here, (peers, channels)),
        ],
        axis=1,
    )
    info = jnp.pad(info, ((0, 0), (0, 6), (0, 0)))
    payload = jnp.concatenate([obs_value[0], info], axis=1)
    payload = to_owners(payload)
    own, slope, norm = forward_call(
        picks, latent, weight, w_in, b_in[None], w_out, b_out[None]
    )
    scale = float(peers * peers * slots)
    grad, loss = score_call(own, swap_members(own), payload, members_all, scale)
    loss_all = to_owners(loss)
    live_total = jnp.sum(payload[:, slots + 1, 0])
    loss_value = jnp.sum(loss_all[:, 0, :]) / (channels * live_total)
    latent_grad = backward_call(picks, grad, slope, norm, w_in, w_out, points)
    return latent_grad, loss_value


def solution(mesh):
    split = Mesh(
        mesh.devices.reshape(mesh.shape["member"], 4, 4, 4),
        ("member", "grid_0", "grid_1", "grid_2"),
    )
    return jax.shard_map(
        device_step,
        mesh=split,
        in_specs=(
            P("member", GRID, None),
            P(GRID, None),
            P(GRID, None, None, None),
            P(GRID, None, None, None),
            P(GRID, None),
            P(),
            P(),
            P(),
            P(),
        ),
        out_specs=(P("member", GRID, None), P()),
        check_vma=False,
    )
```

time: 93.7 us -> 97.3 us (1.038)
  blocking collectives: 0 us -> 49.5 us
  starting transfers between devices: 29 us -> 7.66 us
  local copies, waits for them, and re-layouts: 16.8 us -> 1.45 us
  waiting for transfers between devices: 8.81 us -> 0.01 us
  Pallas kernels: 30.4 us -> 32.2 us
  other arithmetic: 3.89 us -> 2.23 us
    all_to_all x0 -> x2, blocking collectives: none -> 49.5 us  [to_owners(): return lax.all_to_all(value, GRID, split_axis=0, concat_axis=0, tiled=True)]
    all_to_all x3 -> x1, starting transfers between devices: 26.8 us -> 5.44 us  [to_owners(): return lax.all_to_all(value, GRID, split_axis=0, concat_axis=0, tiled=True)]
    unnamed x42 -> x8, local copies, waits for them, and re-layouts: 16.7 us -> 1.32 us
    all_to_all x3 -> x1, waiting for transfers between devices: 8.8 us -> 0.01 us  [to_owners(): return lax.all_to_all(value, GRID, split_axis=0, concat_axis=0, tiled=True)]
    pallas_call x5 -> x3, Pallas kernels: 30.4 us -> 32.2 us  [the longest x1 13.7 us: backward_call(): pl.pallas_call(backward_kernel, in_specs=smem() + left(1) + vmem(1) + lef...]
    concatenate x1, other arithmetic: 1.16 us -> 0.09 us  [device_step(): payload = jnp.concatenate([obs_value[0], info], axis=1)]
    ppermute x2 -> x1, starting transfers between devices: 2.22 us -> 2.23 us  [swap_members(): return lax.ppermute(value, 'member', [(0, 1), (1, 0)])]
  transfers between devices with their start and end apart: 5 -> 2, of which waited for: 1 -> 0; matrix products, arithmetic and copies ran while one was open for 4% -> 2% of each run, Pallas kernels for 29% -> 14%
where the time goes in v3:
time: 97.3 us; the launch traced here: 97 us
  blocking collectives  49.5 us (51%)
  Pallas kernels  32.2 us (33%)
  starting transfers between devices  7.66 us (8%)
  between operations  3.82 us (4%)
  other arithmetic  2.23 us (2%)
  local copies, waits for them, and re-layouts  1.45 us (1%)
    all_to_all x2, blocking collectives, to_owners(): return lax.all_to_all(value, GRID, split_axis=0, concat_axis=0, tiled=True)  49.5 us
    pallas_call x1, Pallas kernels, backward_call(): pl.pallas_call(backward_kernel, in_specs=smem() + left(1) + vmem(1) + lef...  13.7 us
    pallas_call x1, Pallas kernels, forward_call(): pl.pallas_call(forward_kernel, in_specs=smem() + left(3) + vmem(3), out_s...  11.2 us
    pallas_call x1, Pallas kernels, score_call(): pl.pallas_call(functools.partial(score_kernel, members_all=members_all, s...  7.28 us
    all_to_all x1, starting transfers between devices, to_owners(): return lax.all_to_all(value, GRID, split_axis=0, concat_axis=0, tiled=True)  5.44 us
    ppermute x1, starting transfers between devices, swap_members(): return lax.ppermute(value, 'member', [(0, 1), (1, 0)])  2.23 us
  transfers between devices with their start and end apart: 2, of which 0 were waited for; matrix products, arithmetic and copies ran while one was open for 2% of the time, Pallas kernels for 14%

profile of v3, /device:TPU:1, one launch (start us, length us, event | category | flops | bytes accessed | tf_op | source)
XLA Modules:
  0.0 97.0 jit_solution(10793270140553513830)
XLA Ops:
  0.6 24.2 %all_to_all.15.weight = bf16[64,32,128]{2,1,0:T(8,128)(2,1)} all-to-all(bf16[64,32,128]{2,1,0:T(8,128)(2,1)} %bitcast.8), channel_id=1, replica_groups=mesh['member'=2,'grid_0'=4,'grid_1'=4,'grid_2'=4] {'grid_0','grid_1','gr..., dimensions={0} | all-to-all | bytes 1048576 | tf_op jit(solution)/shard_map/all_to_all | solution.py:399
  24.9 0.0 copy-start.3
  24.9 0.0 copy-start.2
  24.9 11.2 %forward.1 = (f32[2,64,32,128]{3,2,1,0:T(8,128)}, bf16[2,64,32,512]{3,2,1,0:T(8,128)(2,1)}, bf16[64,32,128]{2,1,0:T(8,128)(2,1)}) custom-call(s32[64]{0:T(128)} %bitcast.9, bf16[2,2048,512]{2,1,0:T(8,128)(2,1)} %latent.1, bf16[64,32,128]{2,1,0:T(8,128)(2,1)} %all_to_all.15.weight, bf16[512,512]{1,0:T(8,128)(2,1)} %w_in.3, f32[1,512]{1,0:T(1,128)} %bitcast.11, ...), custom_call_target="tpu_custom_call" | custom-call | flops 3221225472 | bytes 10485760 | tf_op jit(solution)/shard_map/forward/pallas_call | solution.py:296
  36.1 2.2 %collective-permute-start = (f32[2,64,32,128]{3,2,1,0:T(8,128)}, f32[2,64,32,128]{3,2,1,0:T(8,128)S(1)}, u32[]{:S(2)}, u32[]{:S(2)}) collective-permute-start(f32[2,64,32,128]{3,2,1,0:T(8,128)} %get-tuple-element.7.own), channel_id=1, source_target_pairs={{0,64},{64,0},{1,65},{65,1},{2,66},{66,2},{3,67},{67,3},{4,68},{68... | collective-permute-start | bytes 6291464 | tf_op jit(solution)/shard_map/ppermute | solution.py:395
  38.3 0.0 copy-done.3
  38.3 0.6 minimum_reduce_fusion
  39.6 0.1 stack_broadcast_in_dim.2
  39.8 0.0 copy-done.2
  39.8 0.1 pad_maximum_fusion
  39.9 25.3 %all_to_all.16.payload = f32[64,40,128]{2,1,0:T(8,128)S(1)} all-to-all(f32[64,40,128]{2,1,0:T(8,128)S(1)} %pad_maximum_fusion), channel_id=1, replica_groups=mesh['member'=2,'grid_0'=4,'grid_1'=4,'grid_2'=4] {'grid_0','grid_1','gr..., dimensions={0} | all-to-all | bytes 2621440 | tf_op jit(solution)/shard_map/all_to_all | solution.py:399
  65.2 0.0 copy-start
  65.2 0.8 slice_reduce_fusion
  66.7 0.0 collective-permute-done.other
  66.7 0.0 copy-done
  66.7 0.0 copy-start.1
  66.7 1.3 %copy-done.1 = f32[2,64,32,128]{3,2,1,0:T(8,128)} copy-done((f32[2,64,32,128]{3,2,1,0:T(8,128)}, f32[2,64,32,128]{3,2,1,0:T(8,128)S(1)}, u32[]{:S(2)}) %copy-start.1) | copy-done | bytes 2097176
  68.0 7.3 %score.1 = (bf16[2,64,32,128]{3,2,1,0:T(8,128)(2,1)}, f32[64,8,128]{2,1,0:T(8,128)}) custom-call(f32[2,64,32,128]{3,2,1,0:T(8,128)} %get-tuple-element.7.own, f32[2,64,32,128]{3,2,1,0:T(8,128)} %copy-done.1, f32[64,40,128]{2,1,0:T(8,128)} %copy-done), custom_call_target="tpu_custom_call" | custom-call | flops 20971520 | bytes 6291456 | tf_op jit(solution)/shard_map/score/pallas_call | solution.py:333
  75.3 5.4 %all-to-all-start.2 = ((f32[64,8,128]{2,1,0:T(8,128)}), f32[64,8,128]{2,1,0:T(8,128)S(1)}, u32[]{:S(2)}, u32[]{:S(2)}) async-start(f32[64,8,128]{2,1,0:T(8,128)} %get-tuple-element.11), calls=%async_computation.2 | async-start | bytes 524288 | tf_op jit(solution)/shard_map/all_to_all | solution.py:399
  80.8 13.7 %backward.1 = f32[2,2048,512]{2,1,0:T(8,128)} custom-call(s32[64]{0:T(128)} %bitcast.10, bf16[512,512]{1,0:T(8,128)(2,1)} %w_in.3, bf16[512,128]{1,0:T(8,128)(2,1)} %w_out.3, bf16[2,64,32,128]{3,2,1,0:T(8,128)(2,1)} %get-tuple-element.8.grad, bf16[2,64,32,512]{3,2,1,0:T(8,128)(2,1)} %get-tuple-element.9.slope, bf16[64,32,128]{2,1,0:T(8,128)(2,1)} %get-tuple-element.10.norm), custom_call_target="tpu_custom_call" | custom-call | flops 3221225472 | bytes 13631488 | tf_op jit(solution)/shard_map/backward/pallas_call | solution.py:367
  94.5 0.0 all-to-all-done.2
  94.5 0.7 slice_reduce_fusion.1
  (1 shorter events, 0.0 us)
Async XLA Ops:
  24.9 13.5 %copy-start.3 = (s32[1,64]{1,0:T(1,128)S(1)}, s32[1,64]{1,0:T(1,128)}, u32[]{:S(2)}) copy-start(s32[1,64]{1,0:T(1,128)} %param.13) | copy-start | bytes 772
  24.9 14.9 %copy-start.2 = (f32[1,64,32,128]{3,2,1,0:T(8,128)S(1)}, f32[1,64,32,128]{3,2,1,0:T(8,128)}, u32[]{:S(2)}) copy-start(f32[1,64,32,128]{3,2,1,0:T(8,128)} %param.12) | copy-start | bytes 3145732
  36.1 30.6 %collective-permute-start = (f32[2,64,32,128]{3,2,1,0:T(8,128)}, f32[2,64,32,128]{3,2,1,0:T(8,128)S(1)}, u32[]{:S(2)}, u32[]{:S(2)}) collective-permute-start(f32[2,64,32,128]{3,2,1,0:T(8,128)} %get-tuple-element.7.own), channel_id=1, source_target_pairs={{0,64},{64,0},{1,65},{65,1},{2,66},{66,2},{3,67},{67,3},{4,68},{68... | collective-permute-start | bytes 6291464 | tf_op jit(solution)/shard_map/ppermute | solution.py:395
  65.2 1.5 %copy-start = (f32[64,40,128]{2,1,0:T(8,128)}, f32[64,40,128]{2,1,0:T(8,128)S(1)}, u32[]{:S(2)}) copy-start(f32[64,40,128]{2,1,0:T(8,128)S(1)} %all_to_all.16.payload) | copy-start | bytes 3932164
  66.7 1.3 %copy-start.1 = (f32[2,64,32,128]{3,2,1,0:T(8,128)}, f32[2,64,32,128]{3,2,1,0:T(8,128)S(1)}, u32[]{:S(2)}) copy-start(f32[2,64,32,128]{3,2,1,0:T(8,128)S(1)} %collective-permute-done.other) | copy-start | bytes 6291460
  75.3 19.2 %all-to-all-start.2 = ((f32[64,8,128]{2,1,0:T(8,128)}), f32[64,8,128]{2,1,0:T(8,128)S(1)}, u32[]{:S(2)}, u32[]{:S(2)}) async-start(f32[64,8,128]{2,1,0:T(8,128)} %get-tuple-element.11), calls=%async_computation.2 | async-start | bytes 524288 | tf_op jit(solution)/shard_map/all_to_all | solution.py:399

commit v4 on v3

--- a/solution.py
+++ b/solution.py
@@ -105,9 +105,11 @@
 
 
 def score_kernel(
+    member,
     own,
     other,
     payload,
+    payload_other,
     grad,
     loss,
     own_here,
@@ -129,17 +131,34 @@
         here = pl.ds(step * SCORE_GROUP, SCORE_GROUP)
         return pltpu.make_async_copy(source.at[:, here], target.at[:, here], sem.at[step])
 
-    fetch_payload = pltpu.make_async_copy(payload, payload_here, payload_sem)
-    fetch_payload.start()
+    share = payload.shape[1] - 8
+
+    def fetch_values(source, position, sem):
+        first = pl.multiple_of(position * share, 8)
+        return pltpu.make_async_copy(
+            source.at[:, pl.ds(0, share)],
+            payload_here.at[:, pl.ds(first, share)],
+            payload_sem.at[sem],
+        )
+
+    me = member[0]
+    fetch_info = pltpu.make_async_copy(
+        payload.at[:, pl.ds(share, 8)], payload_here.at[:, pl.ds(slots, 8)], payload_sem.at[2]
+    )
+    fetch_info.start()
+    fetch_values(payload, me, 0).start()
+    fetch_values(payload_other, 1 - me, 1).start()
     for step in range(steps):
         fetch(own, own_here, own_sem, step).start()
         fetch(other, other_here, other_sem, step).start()
-    fetch_payload.wait()
+    fetch_info.wait()
     live_total = jnp.sum(payload_here[:, slots + 1, :], axis=0, keepdims=True)
     factor = scale / live_total
     slot = lax.broadcasted_iota(jnp.int32, (SCORE_GROUP, slots, channels), 1).astype(jnp.float32)
     obs_scale = 1.0 / members_all
     pair_scale = 1.0 / (members_all * (members_all - 1.0))
+    fetch_values(payload, me, 0).wait()
+    fetch_values(payload_other, 1 - me, 1).wait()
 
     def soft(value):
         square = value * value + SOFTEN * SOFTEN
@@ -176,7 +195,8 @@
 
     total = lax.fori_loop(0, steps, body, jnp.zeros((8, channels), jnp.float32))
     total = jnp.sum(total, axis=0, keepdims=True)
-    loss[...] = jnp.broadcast_to(total[None], loss.shape)
+    row = lax.broadcasted_iota(jnp.int32, loss.shape, 1)
+    loss[...] = jnp.where(row == 0, total[None], live_total[None])
     for step in range(steps):
         fetch(grad_here, grad, grad_sem, step).wait()
 
@@ -326,13 +346,13 @@
     )(picks, latent, weight, w_in, b_in, w_out, b_out)
 
 
-def score_call(own, other, payload, members_all, scale):
+def score_call(member, own, other, payload, payload_other, members_all, scale):
     members, peers, slots, channels = own.shape
     rows = members * peers * slots
     steps = peers // SCORE_GROUP
     return pl.pallas_call(
         functools.partial(score_kernel, members_all=members_all, scale=scale),
-        in_specs=left(3),
+        in_specs=smem() + left(4),
         out_specs=left(1) + vmem(1),
         out_shape=[
             jax.ShapeDtypeStruct(own.shape, jnp.bfloat16),
@@ -341,11 +361,11 @@
         scratch_shapes=[
             pltpu.VMEM(own.shape, jnp.float32),
             pltpu.VMEM(own.shape, jnp.float32),
-            pltpu.VMEM(payload.shape, jnp.float32),
+            pltpu.VMEM((peers, slots + 8, channels), jnp.float32),
             pltpu.VMEM(own.shape, jnp.bfloat16),
             dma(steps),
             dma(steps),
-            dma(),
+            dma(3),
             dma(steps),
         ],
         cost_estimate=pl.CostEstimate(
@@ -354,7 +374,7 @@
             transcendentals=rows * channels * 5,
         ),
         name="score",
-    )(own, other, payload)
+    )(member, own, other, payload, payload_other)
 
 
 def backward_call(picks, grad, slope, norm, w_in, w_out, points):
@@ -416,16 +436,26 @@
         axis=1,
     )
     info = jnp.pad(info, ((0, 0), (0, 6), (0, 0)))
-    payload = jnp.concatenate([obs_value[0], info], axis=1)
+    member = lax.axis_index("member")
+    share = slots // lax.axis_size("member")
+    values = lax.dynamic_slice_in_dim(obs_value[0], member * share, share, axis=1)
+    payload = jnp.concatenate([values, info], axis=1)
     payload = to_owners(payload)
     own, slope, norm = forward_call(
         picks, latent, weight, w_in, b_in[None], w_out, b_out[None]
     )
     scale = float(peers * peers * slots)
-    grad, loss = score_call(own, swap_members(own), payload, members_all, scale)
+    grad, loss = score_call(
+        jnp.full((1,), member, jnp.int32),
+        own,
+        swap_members(own),
+        payload,
+        swap_members(payload),
+        members_all,
+        scale,
+    )
     loss_all = to_owners(loss)
-    live_total = jnp.sum(payload[:, slots + 1, 0])
-    loss_value = jnp.sum(loss_all[:, 0, :]) / (channels * live_total)
+    loss_value = jnp.sum(loss_all[:, 0, :]) / (channels * loss_all[0, 1, 0])
     latent_grad = backward_call(picks, grad, slope, norm, w_in, w_out, points)
     return latent_grad, loss_value
 

time: 97.3 us -> 93.8 us (0.964)
  blocking collectives: 49.5 us -> 44.2 us
  waiting for transfers between devices: 0.01 us -> 1.92 us
    all_to_all x2, blocking collectives: 49.5 us -> 44.2 us  [to_owners(): return lax.all_to_all(value, GRID, split_axis=0, concat_axis=0, tiled=True)]
    ppermute x1 -> x2, waiting for transfers between devices: 0.01 us -> 1.91 us  [swap_members(): return lax.ppermute(value, 'member', [(0, 1), (1, 0)])]
    ppermute x1 -> x2, starting transfers between devices: 2.23 us -> 3.73 us  [swap_members(): return lax.ppermute(value, 'member', [(0, 1), (1, 0)])]
  transfers between devices with their start and end apart: 2 -> 3, of which waited for: 0 -> 1; matrix products, arithmetic and copies ran while one was open for 2% -> 1% of each run, Pallas kernels for 14% -> 15%
where the time goes in v4:
time: 93.8 us; the launch traced here: 93.4 us
  blocking collectives  44.2 us (47%)
  Pallas kernels  32.1 us (34%)
  starting transfers between devices  8.36 us (9%)
  between operations  3.78 us (4%)
  waiting for transfers between devices  1.92 us (2%)
  local copies, waits for them, and re-layouts  1.64 us (2%)
  other arithmetic  1.44 us (2%)
    all_to_all x2, blocking collectives, to_owners(): return lax.all_to_all(value, GRID, split_axis=0, concat_axis=0, tiled=True)  44.2 us
    pallas_call x1, Pallas kernels, backward_call(): pl.pallas_call(backward_kernel, in_specs=smem() + left(1) + vmem(1) + lef...  13.7 us
    pallas_call x1, Pallas kernels, forward_call(): pl.pallas_call(forward_kernel, in_specs=smem() + left(3) + vmem(3), out_s...  11.2 us
    pallas_call x1, Pallas kernels, score_call(): pl.pallas_call(functools.partial(score_kernel, members_all=members_all, s...  7.17 us
    all_to_all x1, starting transfers between devices, to_owners(): return lax.all_to_all(value, GRID, split_axis=0, concat_axis=0, tiled=True)  4.62 us
    ppermute x2, starting transfers between devices, swap_members(): return lax.ppermute(value, 'member', [(0, 1), (1, 0)])  3.73 us
    ppermute x2, waiting for transfers between devices, swap_members(): return lax.ppermute(value, 'member', [(0, 1), (1, 0)])  1.91 us
  transfers between devices with their start and end apart: 3, of which 1 were waited for; matrix products, arithmetic and copies ran while one was open for 1% of the time, Pallas kernels for 15%

profile of v4, /device:TPU:1, one launch (start us, length us, event | category | flops | bytes accessed | tf_op | source)
XLA Modules:
  0.0 93.4 jit_solution(1563211869329293022)
XLA Ops:
  0.6 0.0 copy-start
  0.6 24.4 %all_to_all.15.weight = bf16[64,32,128]{2,1,0:T(8,128)(2,1)} all-to-all(bf16[64,32,128]{2,1,0:T(8,128)(2,1)} %bitcast.10), channel_id=1, replica_groups=mesh['member'=2,'grid_0'=4,'grid_1'=4,'grid_2'=4] {'grid_0','grid_1','gr..., dimensions={0} | all-to-all | bytes 1048576 | tf_op jit(solution)/shard_map/all_to_all | solution.py:419
  25.0 0.0 copy-start.3
  25.0 11.2 %forward.1 = (f32[2,64,32,128]{3,2,1,0:T(8,128)}, bf16[2,64,32,512]{3,2,1,0:T(8,128)(2,1)}, bf16[64,32,128]{2,1,0:T(8,128)(2,1)}) custom-call(s32[64]{0:T(128)} %bitcast.11, bf16[2,2048,512]{2,1,0:T(8,128)(2,1)} %latent.1, bf16[64,32,128]{2,1,0:T(8,128)(2,1)} %all_to_all.15.weight, bf16[512,512]{1,0:T(8,128)(2,1)} %w_in.3, f32[1,512]{1,0:T(1,128)} %bitcast.13, ...), custom_call_target="tpu_custom_call" | custom-call | flops 3221225472 | bytes 10485760 | tf_op jit(solution)/shard_map/forward/pallas_call | solution.py:316
  36.2 2.2 %collective-permute-start = (f32[2,64,32,128]{3,2,1,0:T(8,128)}, f32[2,64,32,128]{3,2,1,0:T(8,128)}, u32[]{:S(2)}, u32[]{:S(2)}) collective-permute-start(f32[2,64,32,128]{3,2,1,0:T(8,128)} %get-tuple-element.7.own), channel_id=1, source_target_pairs={{0,64},{64,0},{1,65},{65,1},{2,66},{66,2},{3,67},{67,3},{4,68},{68... | collective-permute-start | bytes 6291464 | tf_op jit(solution)/shard_map/ppermute | solution.py:415
  38.4 0.0 copy-done.3
  38.4 0.7 minimum_reduce_fusion
  39.7 0.1 stack_broadcast_in_dim.2
  39.9 0.0 copy-done
  40.0 0.1 pad_maximum_fusion
  40.0 19.8 %all_to_all.16.payload = f32[64,24,128]{2,1,0:T(8,128)S(1)} all-to-all(f32[64,24,128]{2,1,0:T(8,128)S(1)} %pad_maximum_fusion), channel_id=1, replica_groups=mesh['member'=2,'grid_0'=4,'grid_1'=4,'grid_2'=4] {'grid_0','grid_1','gr..., dimensions={0} | all-to-all | bytes 1572864 | tf_op jit(solution)/shard_map/all_to_all | solution.py:419
  59.8 0.0 copy-start.1
  59.8 1.5 %collective-permute-start.1 = (f32[64,24,128]{2,1,0:T(8,128)S(1)}, f32[64,24,128]{2,1,0:T(8,128)S(1)}, u32[]{:S(2)}, u32[]{:S(2)}) collective-permute-start(f32[64,24,128]{2,1,0:T(8,128)S(1)} %all_to_all.16.payload), channel_id=1, source_target_pairs={{0,64},{64,0},{1,65},{65,1},{2,66},{66,2},{3,67},{67,3},{4,68},{68... | collective-permute-start | bytes 2359304 | tf_op jit(solution)/shard_map/ppermute | solution.py:415
  61.4 1.9 %collective-permute-done.1.payload_other = f32[64,24,128]{2,1,0:T(8,128)S(1)} collective-permute-done((f32[64,24,128]{2,1,0:T(8,128)S(1)}, f32[64,24,128]{2,1,0:T(8,128)S(1)}, u32[]{:S(2)}, u32[]{:S(2)}) %collective-permute-start.1) | collective-permute-done | bytes 786464 | tf_op jit(solution)/shard_map/ppermute | solution.py:415
  63.3 0.0 copy-start.2
  63.3 0.0 collective-permute-done.other
  63.3 0.0 copy-done.1
  63.3 0.9 %copy-done.2 = f32[64,24,128]{2,1,0:T(8,128)} copy-done((f32[64,24,128]{2,1,0:T(8,128)}, f32[64,24,128]{2,1,0:T(8,128)S(1)}, u32[]{:S(2)}) %copy-start.2) | copy-done | bytes 786456
  64.2 7.2 %score.1 = (bf16[2,64,32,128]{3,2,1,0:T(8,128)(2,1)}, f32[64,8,128]{2,1,0:T(8,128)}) custom-call(s32[1]{0:T(128)} %bitcast.1.member, f32[2,64,32,128]{3,2,1,0:T(8,128)} %get-tuple-element.7.own, f32[2,64,32,128]{3,2,1,0:T(8,128)} %collective-permute-done.other, f32[64,24,128]{2,1,0:T(8,128)} %copy-done.1, f32[64,24,128]{2,1,0:T(8,128)} %copy-done.2), custom_call_target="tpu_custom_call" | custom-call | flops 20971520 | bytes 6291456 | tf_op jit(solution)/shard_map/score/pallas_call | solution.py:353
  71.4 4.6 %all-to-all-start.2 = ((f32[64,8,128]{2,1,0:T(8,128)}), f32[64,8,128]{2,1,0:T(8,128)S(1)}, u32[]{:S(2)}, u32[]{:S(2)}) async-start(f32[64,8,128]{2,1,0:T(8,128)} %get-tuple-element.11), calls=%async_computation.2 | async-start | bytes 524288 | tf_op jit(solution)/shard_map/all_to_all | solution.py:419
  76.0 13.7 %backward.1 = f32[2,2048,512]{2,1,0:T(8,128)} custom-call(s32[64]{0:T(128)} %bitcast.12, bf16[512,512]{1,0:T(8,128)(2,1)} %w_in.3, bf16[512,128]{1,0:T(8,128)(2,1)} %w_out.3, bf16[2,64,32,128]{3,2,1,0:T(8,128)(2,1)} %get-tuple-element.8.grad, bf16[2,64,32,512]{3,2,1,0:T(8,128)(2,1)} %get-tuple-element.9.slope, bf16[64,32,128]{2,1,0:T(8,128)(2,1)} %get-tuple-element.10.norm), custom_call_target="tpu_custom_call" | custom-call | flops 3221225472 | bytes 13631488 | tf_op jit(solution)/shard_map/backward/pallas_call | solution.py:387
  89.8 0.0 all-to-all-done.2
  89.8 0.5 slice.9
  91.0 0.7 slice_reduce_fusion
  (2 shorter events, 0.1 us)
Async XLA Ops:
  0.6 39.3 %copy-start = (f32[1,64,32,128]{3,2,1,0:T(8,128)S(1)}, f32[1,64,32,128]{3,2,1,0:T(8,128)}, u32[]{:S(2)}) copy-start(f32[1,64,32,128]{3,2,1,0:T(8,128)} %param.12) | copy-start | bytes 3145732
  25.0 13.4 %copy-start.3 = (s32[1,64]{1,0:T(1,128)S(1)}, s32[1,64]{1,0:T(1,128)}, u32[]{:S(2)}) copy-start(s32[1,64]{1,0:T(1,128)} %param.13) | copy-start | bytes 772
  36.2 27.1 %collective-permute-start = (f32[2,64,32,128]{3,2,1,0:T(8,128)}, f32[2,64,32,128]{3,2,1,0:T(8,128)}, u32[]{:S(2)}, u32[]{:S(2)}) collective-permute-start(f32[2,64,32,128]{3,2,1,0:T(8,128)} %get-tuple-element.7.own), channel_id=1, source_target_pairs={{0,64},{64,0},{1,65},{65,1},{2,66},{66,2},{3,67},{67,3},{4,68},{68... | collective-permute-start | bytes 6291464 | tf_op jit(solution)/shard_map/ppermute | solution.py:415
  59.8 3.4 %copy-start.1 = (f32[64,24,128]{2,1,0:T(8,128)}, f32[64,24,128]{2,1,0:T(8,128)S(1)}, u32[]{:S(2)}) copy-start(f32[64,24,128]{2,1,0:T(8,128)S(1)} %all_to_all.16.payload) | copy-start | bytes 2359300
  59.8 3.4 %collective-permute-start.1 = (f32[64,24,128]{2,1,0:T(8,128)S(1)}, f32[64,24,128]{2,1,0:T(8,128)S(1)}, u32[]{:S(2)}, u32[]{:S(2)}) collective-permute-start(f32[64,24,128]{2,1,0:T(8,128)S(1)} %all_to_all.16.payload), channel_id=1, source_target_pairs={{0,64},{64,0},{1,65},{65,1},{2,66},{66,2},{3,67},{67,3},{4,68},{68... | collective-permute-start | bytes 2359304 | tf_op jit(solution)/shard_map/ppermute | solution.py:415
  63.3 1.0 %copy-start.2 = (f32[64,24,128]{2,1,0:T(8,128)}, f32[64,24,128]{2,1,0:T(8,128)S(1)}, u32[]{:S(2)}) copy-start(f32[64,24,128]{2,1,0:T(8,128)S(1)} %collective-permute-done.1.payload_other) | copy-start | bytes 2359300
  71.4 18.4 %all-to-all-start.2 = ((f32[64,8,128]{2,1,0:T(8,128)}), f32[64,8,128]{2,1,0:T(8,128)S(1)}, u32[]{:S(2)}, u32[]{:S(2)}) async-start(f32[64,8,128]{2,1,0:T(8,128)} %get-tuple-element.11), calls=%async_computation.2 | async-start | bytes 524288 | tf_op jit(solution)/shard_map/all_to_all | solution.py:419

commit v5 on v3

--- a/solution.py
+++ b/solution.py
@@ -175,7 +175,7 @@
         return total + jnp.sum((per_obs * live).reshape(-1, 8, channels), axis=0)
 
     total = lax.fori_loop(0, steps, body, jnp.zeros((8, channels), jnp.float32))
-    total = jnp.sum(total, axis=0, keepdims=True)
+    total = jnp.sum(total, axis=0, keepdims=True) / (channels * live_total)
     loss[...] = jnp.broadcast_to(total[None], loss.shape)
     for step in range(steps):
         fetch(grad_here, grad, grad_sem, step).wait()
@@ -216,8 +216,13 @@
             slope.at[m, pl.ds(begin, half)], slope_here.at[step], slope_sem.at[step]
         )
 
-    def put(m):
-        return pltpu.make_async_copy(total.at[m], out.at[m], out_sem.at[m])
+    part_width = width // HALVES
+
+    def put(m, part):
+        columns = pl.ds(part * part_width, part_width)
+        return pltpu.make_async_copy(
+            total.at[m, :, columns], out.at[m, :, columns], out_sem.at[m, part]
+        )
 
     fetch_w_in = pltpu.make_async_copy(w_in, w_in_here, w_in_sem)
     fetch_norm = pltpu.make_async_copy(norm, norm_here, norm_sem)
@@ -250,24 +255,27 @@
             preferred_element_type=jnp.float32,
         )
         rows[...] = grad_interp.astype(jnp.bfloat16).reshape(half, slots, width)
-        for d in range(half):
-            start = pl.multiple_of(picks[begin + d] * block, block)
-            total[m, pl.ds(start, block), :] += lax.dot_general(
-                norm_here[begin + d],
-                rows[d],
-                (((0,), (0,)), ((), ())),
-                preferred_element_type=jnp.float32,
-            )
-
-        @pl.when(step % HALVES == HALVES - 1)
-        def _():
-            put(m).start()
+        for part in range(HALVES):
+            columns = pl.ds(part * part_width, part_width)
+            for d in range(half):
+                start = pl.multiple_of(picks[begin + d] * block, block)
+                total[m, pl.ds(start, block), columns] += lax.dot_general(
+                    norm_here[begin + d],
+                    rows[d, :, columns],
+                    (((0,), (0,)), ((), ())),
+                    preferred_element_type=jnp.float32,
+                )
+
+            @pl.when(step % HALVES == HALVES - 1)
+            def _(part=part):
+                put(m, part).start()
 
         return carry
 
     lax.fori_loop(0, members * HALVES, body, 0)
     for m in range(members):
-        put(m).wait()
+        for part in range(HALVES):
+            put(m, part).wait()
 
 
 def vmem(count):
@@ -376,7 +384,7 @@
             pltpu.VMEM((steps, half, slots, inner), jnp.bfloat16),
             pltpu.VMEM(norm.shape, jnp.bfloat16),
             dma(),
-            dma(members),
+            dma(members, HALVES),
             dma(steps),
             dma(steps),
             dma(),
@@ -424,8 +432,7 @@
     scale = float(peers * peers * slots)
     grad, loss = score_call(own, swap_members(own), payload, members_all, scale)
     loss_all = to_owners(loss)
-    live_total = jnp.sum(payload[:, slots + 1, 0])
-    loss_value = jnp.sum(loss_all[:, 0, :]) / (channels * live_total)
+    loss_value = jnp.sum(loss_all[:, 0, :])
     latent_grad = backward_call(picks, grad, slope, norm, w_in, w_out, points)
     return latent_grad, loss_value
 

time: 97.3 us -> 93.8 us (0.964)
  between operations: 3.82 us -> 1.36 us
  transfers between devices with their start and end apart: 2 -> 2, of which waited for: 0 -> 0; matrix products, arithmetic and copies ran while one was open for 2% -> 1% of each run, Pallas kernels for 14% -> 14%
where the time goes in v5:
time: 93.8 us; the launch traced here: 93.5 us
  blocking collectives  49.8 us (53%)
  Pallas kernels  31.8 us (34%)
  starting transfers between devices  7.66 us (8%)
  local copies, waits for them, and re-layouts  1.44 us (2%)
  other arithmetic  1.42 us (2%)
  between operations  1.36 us (1%)
    all_to_all x2, blocking collectives, to_owners(): return lax.all_to_all(value, GRID, split_axis=0, concat_axis=0, tiled=True)  49.8 us
    pallas_call x1, Pallas kernels, backward_call(): pl.pallas_call(backward_kernel, in_specs=smem() + left(1) + vmem(1) + lef...  13.2 us
    pallas_call x1, Pallas kernels, forward_call(): pl.pallas_call(forward_kernel, in_specs=smem() + left(3) + vmem(3), out_s...  11.2 us
    pallas_call x1, Pallas kernels, score_call(): pl.pallas_call(functools.partial(score_kernel, members_all=members_all, s...  7.28 us
    all_to_all x1, starting transfers between devices, to_owners(): return lax.all_to_all(value, GRID, split_axis=0, concat_axis=0, tiled=True)  5.44 us
    ppermute x1, starting transfers between devices, swap_members(): return lax.ppermute(value, 'member', [(0, 1), (1, 0)])  2.23 us
  transfers between devices with their start and end apart: 2, of which 0 were waited for; matrix products, arithmetic and copies ran while one was open for 1% of the time, Pallas kernels for 14%

profile of v5, /device:TPU:1, one launch (start us, length us, event | category | flops | bytes accessed | tf_op | source)
XLA Modules:
  0.0 93.5 jit_solution(8329407114345133423)
XLA Ops:
  0.6 24.2 %all_to_all.15.weight = bf16[64,32,128]{2,1,0:T(8,128)(2,1)} all-to-all(bf16[64,32,128]{2,1,0:T(8,128)(2,1)} %bitcast.8), channel_id=1, replica_groups=mesh['member'=2,'grid_0'=4,'grid_1'=4,'grid_2'=4] {'grid_0','grid_1','gr..., dimensions={0} | all-to-all | bytes 1048576 | tf_op jit(solution)/shard_map/all_to_all | solution.py:407
  24.9 0.0 copy-start.2
  24.9 0.0 copy-start.1
  24.9 11.2 %forward.1 = (f32[2,64,32,128]{3,2,1,0:T(8,128)}, bf16[2,64,32,512]{3,2,1,0:T(8,128)(2,1)}, bf16[64,32,128]{2,1,0:T(8,128)(2,1)}) custom-call(s32[64]{0:T(128)} %bitcast.9, bf16[2,2048,512]{2,1,0:T(8,128)(2,1)} %latent.1, bf16[64,32,128]{2,1,0:T(8,128)(2,1)} %all_to_all.15.weight, bf16[512,512]{1,0:T(8,128)(2,1)} %w_in.3, f32[1,512]{1,0:T(1,128)} %bitcast.11, ...), custom_call_target="tpu_custom_call" | custom-call | flops 3221225472 | bytes 10485760 | tf_op jit(solution)/shard_map/forward/pallas_call | solution.py:304
  36.1 2.2 %collective-permute-start = (f32[2,64,32,128]{3,2,1,0:T(8,128)}, f32[2,64,32,128]{3,2,1,0:T(8,128)S(1)}, u32[]{:S(2)}, u32[]{:S(2)}) collective-permute-start(f32[2,64,32,128]{3,2,1,0:T(8,128)} %get-tuple-element.7.own), channel_id=1, source_target_pairs={{0,64},{64,0},{1,65},{65,1},{2,66},{66,2},{3,67},{67,3},{4,68},{68... | collective-permute-start | bytes 6291464 | tf_op jit(solution)/shard_map/ppermute | solution.py:403
  38.3 0.0 copy-done.2
  38.3 0.6 minimum_reduce_fusion
  39.6 0.1 stack_broadcast_in_dim.2
  39.8 0.0 copy-done.1
  39.8 0.1 pad_maximum_fusion
  39.9 25.6 %all_to_all.16.payload = f32[64,40,128]{2,1,0:T(8,128)} all-to-all(f32[64,40,128]{2,1,0:T(8,128)S(1)} %pad_maximum_fusion), channel_id=1, replica_groups=mesh['member'=2,'grid_0'=4,'grid_1'=4,'grid_2'=4] {'grid_0','grid_1','gr..., dimensions={0} | all-to-all | bytes 2621440 | tf_op jit(solution)/shard_map/all_to_all | solution.py:407
  65.5 0.0 collective-permute-done.other
  65.5 0.0 copy-start
  65.5 1.3 %copy-done = f32[2,64,32,128]{3,2,1,0:T(8,128)} copy-done((f32[2,64,32,128]{3,2,1,0:T(8,128)}, f32[2,64,32,128]{3,2,1,0:T(8,128)S(1)}, u32[]{:S(2)}) %copy-start) | copy-done | bytes 2097176
  66.8 7.3 %score.1 = (bf16[2,64,32,128]{3,2,1,0:T(8,128)(2,1)}, f32[64,8,128]{2,1,0:T(8,128)}) custom-call(f32[2,64,32,128]{3,2,1,0:T(8,128)} %get-tuple-element.7.own, f32[2,64,32,128]{3,2,1,0:T(8,128)} %copy-done, f32[64,40,128]{2,1,0:T(8,128)} %all_to_all.16.payload), custom_call_target="tpu_custom_call" | custom-call | flops 20971520 | bytes 6291456 | tf_op jit(solution)/shard_map/score/pallas_call | solution.py:341
  74.1 5.4 %all-to-all-start.2 = ((f32[64,8,128]{2,1,0:T(8,128)}), f32[64,8,128]{2,1,0:T(8,128)S(1)}, u32[]{:S(2)}, u32[]{:S(2)}) async-start(f32[64,8,128]{2,1,0:T(8,128)} %get-tuple-element.11), calls=%async_computation.2 | async-start | bytes 524288 | tf_op jit(solution)/shard_map/all_to_all | solution.py:407
  79.5 13.2 %backward.1 = f32[2,2048,512]{2,1,0:T(8,128)} custom-call(s32[64]{0:T(128)} %bitcast.10, bf16[512,512]{1,0:T(8,128)(2,1)} %w_in.3, bf16[512,128]{1,0:T(8,128)(2,1)} %w_out.3, bf16[2,64,32,128]{3,2,1,0:T(8,128)(2,1)} %get-tuple-element.8.grad, bf16[2,64,32,512]{3,2,1,0:T(8,128)(2,1)} %get-tuple-element.9.slope, bf16[64,32,128]{2,1,0:T(8,128)(2,1)} %get-tuple-element.10.norm), custom_call_target="tpu_custom_call" | custom-call | flops 3221225472 | bytes 13631488 | tf_op jit(solution)/shard_map/backward/pallas_call | solution.py:375
  92.8 0.0 all-to-all-done.2
  92.8 0.7 slice_reduce_fusion
  (1 shorter events, 0.0 us)
Async XLA Ops:
  24.9 13.5 %copy-start.2 = (s32[1,64]{1,0:T(1,128)S(1)}, s32[1,64]{1,0:T(1,128)}, u32[]{:S(2)}) copy-start(s32[1,64]{1,0:T(1,128)} %param.13) | copy-start | bytes 772
  24.9 14.9 %copy-start.1 = (f32[1,64,32,128]{3,2,1,0:T(8,128)S(1)}, f32[1,64,32,128]{3,2,1,0:T(8,128)}, u32[]{:S(2)}) copy-start(f32[1,64,32,128]{3,2,1,0:T(8,128)} %param.12) | copy-start | bytes 3145732
  36.1 29.4 %collective-permute-start = (f32[2,64,32,128]{3,2,1,0:T(8,128)}, f32[2,64,32,128]{3,2,1,0:T(8,128)S(1)}, u32[]{:S(2)}, u32[]{:S(2)}) collective-permute-start(f32[2,64,32,128]{3,2,1,0:T(8,128)} %get-tuple-element.7.own), channel_id=1, source_target_pairs={{0,64},{64,0},{1,65},{65,1},{2,66},{66,2},{3,67},{67,3},{4,68},{68... | collective-permute-start | bytes 6291464 | tf_op jit(solution)/shard_map/ppermute | solution.py:403
  65.5 1.3 %copy-start = (f32[2,64,32,128]{3,2,1,0:T(8,128)}, f32[2,64,32,128]{3,2,1,0:T(8,128)S(1)}, u32[]{:S(2)}) copy-start(f32[2,64,32,128]{3,2,1,0:T(8,128)S(1)} %collective-permute-done.other) | copy-start | bytes 6291460
  74.1 18.7 %all-to-all-start.2 = ((f32[64,8,128]{2,1,0:T(8,128)}), f32[64,8,128]{2,1,0:T(8,128)S(1)}, u32[]{:S(2)}, u32[]{:S(2)}) async-start(f32[64,8,128]{2,1,0:T(8,128)} %get-tuple-element.11), calls=%async_computation.2 | async-start | bytes 524288 | tf_op jit(solution)/shard_map/all_to_all | solution.py:407
